TPU v7x, 8 devices: a whole 2x2x1 slice. The times are simulated.
8 devices in a mesh: dp: 1 (over z), tp: 8 (over y, x, core).
Axes of the slice: x: 2, y: 2, z: 1, core: 2. Of those that a mesh axis runs over, the one named last changes fastest.
Arguments:
- x: bfloat16 [8192, 3072], P('dp')
- pos: int32 [8192], P('dp')
- g1: bfloat16 [3072], replicated
- g2: bfloat16 [3072], replicated
- wq: bfloat16 [3072, 3072], P(None, 'tp')
- wk: bfloat16 [3072, 1024], replicated
- wv: bfloat16 [3072, 1024], replicated
- wo: bfloat16 [3072, 3072], P('tp')
- wg: bfloat16 [3072, 8192], P(None, 'tp')
- wu: bfloat16 [3072, 8192], P(None, 'tp')
- wd: bfloat16 [8192, 3072], P('tp')
Outputs:
- output 1: bfloat16 [8192, 3072], P('dp')
- output 2: bfloat16 [8192, 8, 128], P('dp', 'tp')
- output 3: bfloat16 [8192, 8, 128], P('dp', 'tp')
All inputs are finite; a program needn't handle non-finite values.
Results may differ from a plain program's by a relative error of at most 0.0156133.
Values are sent between devices in bfloat16 or wider.
A program may use at most 1 GiB of HBM per device.

v0:
```python
import functools

import jax
import jax.numpy as jnp
from jax import lax
from jax.experimental import pallas as pl
from jax.experimental.pallas import tpu as pltpu
from jax.sharding import PartitionSpec as P


HEAD = 128
EPS = 1e-5
ROPE_BASE = 500000.0
LOG2E = 1.4426950408889634
CHUNKS = (2048, 1536, 2048, 1536, 1024)
VMEM = 62 << 20
F32, BF = jnp.float32, jnp.bfloat16


def _cs(pos):
    half = HEAD // 2
    inv = ROPE_BASE ** (-2.0 * jnp.arange(half, dtype=F32) / HEAD)
    ang = pos.astype(F32)[:, None] * inv
    return jnp.cos(ang), jnp.sin(ang)


def _qkv_kernel(hl, x_ref, g_ref, w_ref, c_ref, s_ref, q_ref, k_ref, v_ref):
    x = x_ref[...].astype(F32)
    inv = lax.rsqrt(jnp.mean(x * x, axis=-1, keepdims=True) + EPS)
    a = (x * inv * g_ref[...].astype(F32)).astype(BF)
    r = jnp.dot(a, w_ref[...], preferred_element_type=F32)
    c, s = c_ref[...], s_ref[...]
    cc = jnp.concatenate([c, c], axis=-1)
    ss = jnp.concatenate([-s, s], axis=-1)
    for n in range(hl + 1):
        t = r[:, n * HEAD:(n + 1) * HEAD]
        t = (t * cc + pltpu.roll(t, HEAD // 2, 1) * ss).astype(BF)
        if n < hl:
            q_ref[:, n * HEAD:(n + 1) * HEAD] = t
        else:
            k_ref[...] = t
    v_ref[...] = r[:, (hl + 1) * HEAD:].astype(BF)


def _qkv(x, g1, w, c, s, hl):
    t, d = x.shape
    bm = min(t, 512)
    n = w.shape[1]
    row = lambda i: (i, 0)
    fix = lambda i: (0, 0)
    return pl.pallas_call(
        functools.partial(_qkv_kernel, hl),
        grid=(t // bm,),
        in_specs=[
            pl.BlockSpec((bm, d), row),
            pl.BlockSpec((1, d), fix),
            pl.BlockSpec((d, n), fix),
            pl.BlockSpec((bm, HEAD // 2), row),
            pl.BlockSpec((bm, HEAD // 2), row),
        ],
        out_specs=[
            pl.BlockSpec((bm, hl * HEAD), row),
            pl.BlockSpec((bm, HEAD), row),
            pl.BlockSpec((bm, HEAD), row),
        ],
        out_shape=[
            jax.ShapeDtypeStruct((t, hl * HEAD), BF),
            jax.ShapeDtypeStruct((t, HEAD), BF),
            jax.ShapeDtypeStruct((t, HEAD), BF),
        ],
        compiler_params=pltpu.CompilerParams(vmem_limit_bytes=VMEM),
        cost_estimate=pl.CostEstimate(flops=2 * t * d * n, bytes_accessed=2 * t * d, transcendentals=0),
        name="qkv",
    )(x, g1.reshape(1, d), w, c, s)


def _attn_kernel(hl, q0, bq, bk, q_ref, kt_ref, v_ref, o_ref, m_sc, l_sc, a_sc):
    i = pl.program_id(0)
    row0 = q0 + i * bq
    c = HEAD ** -0.5 * LOG2E
    for h in range(hl):
        m_sc[h] = jnp.full((bq, HEAD), -1e30, F32)
        l_sc[h] = jnp.zeros((bq, HEAD), F32)
        a_sc[h] = jnp.zeros((bq, HEAD), F32)

    def block(j, masked):
        start = pl.multiple_of(j * bk, bk)
        kt = kt_ref[:, pl.ds(start, bk)]
        v = v_ref[pl.ds(start, bk), :]
        scores = []
        for h in range(hl):
            q = q_ref[:, h * HEAD:(h + 1) * HEAD]
            s = jnp.dot(q, kt, preferred_element_type=F32) * c
            if masked:
                rows = row0 + lax.broadcasted_iota(jnp.int32, (bq, bk), 0)
                cols = start + lax.broadcasted_iota(jnp.int32, (bq, bk), 1)
                s = jnp.where(cols <= rows, s, -jnp.inf)
            scores.append(s)
        for h in range(hl):
            s = scores[h]
            m0 = m_sc[h]
            m1 = jnp.maximum(m0, jnp.max(s, axis=-1, keepdims=True))
            p = jnp.exp2(s - jnp.concatenate([m1] * (bk // HEAD), axis=-1))
            al = jnp.exp2(m0 - m1)
            part = p[:, :HEAD]
            for g in range(1, bk // HEAD):
                part = part + p[:, g * HEAD:(g + 1) * HEAD]
            l_sc[h] = l_sc[h] * al + part
            a_sc[h] = a_sc[h] * al + jnp.dot(p.astype(BF), v, preferred_element_type=F32)
            m_sc[h] = m1

    nfull = row0 // bk

    def body(j, carry):
        block(j, False)
        return carry

    lax.fori_loop(0, nfull, body, 0)
    block(nfull, True)
    for h in range(hl):
        l = jnp.sum(l_sc[h], axis=-1, keepdims=True)
        o_ref[:, h * HEAD:(h + 1) * HEAD] = (a_sc[h] / l).astype(BF)


def _attn(q, kt, v, hl, q0, rows):
    t = v.shape[0]
    bq = min(rows, 512)
    bk = bq
    nq = rows // bq
    b0 = q0 // bq
    end = q0 + rows
    area = sum((q0 + (i + 1) * bq) * bq for i in range(nq))
    return pl.pallas_call(
        functools.partial(_attn_kernel, hl, q0, bq, bk),
        grid=(nq,),
        in_specs=[
            pl.BlockSpec((bq, hl * HEAD), lambda i: (b0 + i, 0)),
            pl.BlockSpec((HEAD, t), lambda i: (0, 0)),
            pl.BlockSpec((t, HEAD), lambda i: (0, 0)),
        ],
        out_specs=pl.BlockSpec((bq, hl * HEAD), lambda i: (i, 0)),
        out_shape=jax.ShapeDtypeStruct((rows, hl * HEAD), BF),
        scratch_shapes=[pltpu.VMEM((hl, bq, HEAD), F32)] * 3,
        compiler_params=pltpu.CompilerParams(vmem_limit_bytes=VMEM),
        cost_estimate=pl.CostEstimate(
            flops=4 * 3 * HEAD * hl * area, bytes_accessed=4 * end * HEAD, transcendentals=hl * area),
    )(q, kt, v)


def _h_kernel(n, sizes, off_ref, x_ref, g_ref, *refs):
    o_refs, w_refs = refs[:n], refs[n:n + len(sizes)]
    h_ref, b_ref, w_sc, sem = refs[n + len(sizes):]

    @pl.when(pl.program_id(0) == 0)
    def _():
        copies, at = [], 0
        for i, (w, size) in enumerate(zip(w_refs, sizes)):
            copies.append(pltpu.make_async_copy(w, w_sc.at[pl.ds(at, size), :], sem.at[i]))
            at += size
        for cp in copies:
            cp.start()
        for cp in copies:
            cp.wait()

    o = jnp.concatenate([r[...] for r in o_refs], axis=-1)
    h = (x_ref[...].astype(F32) + jnp.dot(o, w_sc[...], preferred_element_type=F32)).astype(BF)
    h_ref[...] = h
    h = h.astype(F32)
    inv = lax.rsqrt(jnp.mean(h * h, axis=-1, keepdims=True) + EPS)
    b_ref[...] = (h * inv * g_ref[...].astype(F32)).astype(BF)


def _h(start, x, g2, os, ws):
    rows, kk = os[0].shape
    d = x.shape[1]
    n = len(os)
    bm = min(rows, 256)
    sizes = tuple(w.shape[0] for w in ws)
    row = lambda i, o: (i, 0)
    fix = lambda i, o: (0, 0)
    return pl.pallas_call(
        functools.partial(_h_kernel, n, sizes),
        grid_spec=pltpu.PrefetchScalarGridSpec(
            num_scalar_prefetch=1,
            grid=(rows // bm,),
            in_specs=[
                pl.BlockSpec((bm, d), lambda i, o: (o[0] + i, 0)),
                pl.BlockSpec((1, d), fix),
                *[pl.BlockSpec((bm, kk), row) for _ in range(n)],
                *[pl.BlockSpec(memory_space=pl.ANY) for _ in ws],
            ],
            out_specs=[pl.BlockSpec((bm, d), row), pl.BlockSpec((bm, d), row)],
            scratch_shapes=[pltpu.VMEM((n * kk, d), BF), pltpu.SemaphoreType.DMA((len(ws),))],
        ),
        out_shape=[jax.ShapeDtypeStruct((rows, d), BF)] * 2,
        compiler_params=pltpu.CompilerParams(vmem_limit_bytes=VMEM),
        cost_estimate=pl.CostEstimate(
            flops=2 * rows * d * n * kk, bytes_accessed=2 * d * (n * kk + 4 * rows), transcendentals=0),
    )((start // bm).reshape(1), x, g2.reshape(1, d), *os, *ws)


def _mlp_kernel(fb, db, b_ref, wg_ref, wu_ref, wd_ref, p_ref, wg_sc, wu_sc, wd_sc, u_sc, sem):
    d, f = wg_sc.shape
    first = pl.program_id(0) == 0

    def up_copies(j):
        cols = pl.ds(j * fb, fb)
        return (pltpu.make_async_copy(wg_ref.at[:, cols], wg_sc.at[:, cols], sem.at[0, j]),
                pltpu.make_async_copy(wu_ref.at[:, cols], wu_sc.at[:, cols], sem.at[1, j]))

    def down_copy():
        return pltpu.make_async_copy(wd_ref, wd_sc, sem.at[2, 0])

    @pl.when(first)
    def _():
        for j in range(f // fb):
            for cp in up_copies(j):
                cp.start()
        down_copy().start()

    b = b_ref[...]
    for j in range(f // fb):
        @pl.when(first)
        def _():
            for cp in up_copies(j):
                cp.wait()

        cols = slice(j * fb, (j + 1) * fb)
        gt = jnp.dot(b, wg_sc[:, cols], preferred_element_type=F32)
        up = jnp.dot(b, wu_sc[:, cols], preferred_element_type=F32)
        u_sc[:, cols] = (gt * jax.nn.sigmoid(gt) * up).astype(BF)

    @pl.when(first)
    def _():
        down_copy().wait()

    u = u_sc[...]
    for j in range(d // db):
        cols = slice(j * db, (j + 1) * db)
        p_ref[:, cols] = jnp.dot(u, wd_sc[:, cols], preferred_element_type=F32).astype(BF)


def _mlp(b, wg, wu, wd):
    rows, d = b.shape
    f = wg.shape[1]
    bm = next((m for m in (512, 384, 256) if rows % m == 0), rows)
    fb, db = min(f, 512), min(d, 512)
    row = lambda i: (i, 0)
    any_ = pl.BlockSpec(memory_space=pl.ANY)
    return pl.pallas_call(
        functools.partial(_mlp_kernel, fb, db),
        grid=(rows // bm,),
        in_specs=[pl.BlockSpec((bm, d), row), any_, any_, any_],
        out_specs=pl.BlockSpec((bm, d), row),
        out_shape=jax.ShapeDtypeStruct((rows, d), BF),
        scratch_shapes=[pltpu.VMEM((d, f), BF), pltpu.VMEM((d, f), BF), pltpu.VMEM((f, d), BF),
                        pltpu.VMEM((bm, f), BF), pltpu.SemaphoreType.DMA((3, f // fb))],
        compiler_params=pltpu.CompilerParams(vmem_limit_bytes=VMEM),
        cost_estimate=pl.CostEstimate(
            flops=6 * rows * d * f, bytes_accessed=2 * d * (3 * f + 2 * rows), transcendentals=rows * f),
    )(b, wg, wu, wd)


def _sum_kernel(groups, q_ref, *refs):
    at = 0
    outs = refs[sum(groups):]
    for g, out in zip(groups, outs):
        t = refs[at][...].astype(F32)
        for r in refs[at + 1:at + g]:
            t = t + r[...].astype(F32)
        out[...] = t.astype(BF)
        at += g


def _sums(q4, piece, terms):
    d = terms[0][0][0].shape[1]
    bm = min(piece, 64)
    nb = piece // bm
    own = lambda i, q: (i, 0)

    def spec(k):
        if k is None:
            return pl.BlockSpec((bm, d), own)
        return pl.BlockSpec((bm, d), lambda i, q: (q[k] * nb + i, 0))

    flat = [t for group in terms for t in group]
    return pl.pallas_call(
        functools.partial(_sum_kernel, tuple(len(g) for g in terms)),
        grid_spec=pltpu.PrefetchScalarGridSpec(
            num_scalar_prefetch=1,
            grid=(nb,),
            in_specs=[spec(k) for _, k in flat],
            out_specs=[pl.BlockSpec((bm, d), own) for _ in terms],
        ),
        out_shape=[jax.ShapeDtypeStruct((piece, d), BF) for _ in terms],
        compiler_params=pltpu.CompilerParams(vmem_limit_bytes=VMEM),
        cost_estimate=pl.CostEstimate(
            flops=400 * piece * d * len(flat), bytes_accessed=2 * piece * d * len(flat), transcendentals=0),
    )(q4, *[a for a, _ in flat])


def _place_kernel(n, at_ref, *refs):
    src, y_ref, buf, sem = refs[:n], refs[-3], refs[-2], refs[-1]
    piece = buf.shape[1]
    loads = [pltpu.make_async_copy(src[i], buf.at[i], sem.at[0, i]) for i in range(n)]
    for cp in loads:
        cp.start()
    stores = [pltpu.make_async_copy(buf.at[i], y_ref.at[pl.ds(pl.multiple_of(at_ref[i], min(piece, 64)), piece), :], sem.at[1, i])
              for i in range(n)]
    for ld, st in zip(loads, stores):
        ld.wait()
        st.start()
    for st in stores:
        st.wait()


def _place(y, at, pieces, t):
    n = len(pieces)
    piece, d = pieces[0].shape
    extra = [] if y is None else [y]
    any_ = pl.BlockSpec(memory_space=pl.ANY)
    return pl.pallas_call(
        functools.partial(_place_kernel, n),
        grid_spec=pltpu.PrefetchScalarGridSpec(
            num_scalar_prefetch=1,
            grid=(),
            in_specs=[any_] * (n + len(extra)),
            out_specs=any_,
            scratch_shapes=[pltpu.VMEM((n, piece, d), BF), pltpu.SemaphoreType.DMA((2, n))],
        ),
        out_shape=jax.ShapeDtypeStruct((t, d), BF),
        input_output_aliases={n + 1: 0} if extra else {},
        compiler_params=pltpu.CompilerParams(vmem_limit_bytes=VMEM),
        cost_estimate=pl.CostEstimate(flops=800 * n * piece * d, bytes_accessed=4 * n * piece * d, transcendentals=0),
    )(at, *pieces, *extra)


def solution(mesh):
    tp = mesh.shape["tp"]
    assert tp == 8

    def swap(a, bit):
        return lax.ppermute(a, "tp", [(i, i ^ bit) for i in range(tp)])

    core, xs, ys = 1, 2, 4

    def layer(x, pos, g1, g2, wq, wk, wv, wo, wg, wu, wd):
        t, _ = x.shape
        hl = wq.shape[1] // HEAD
        r = lax.axis_index("tp")
        c, q4 = r % 2, r // 2
        chunks = CHUNKS if sum(CHUNKS) == t else tuple(s * t // 8192 for s in CHUNKS)
        q0s = [sum(chunks[:n]) for n in range(len(chunks))]
        qs = jnp.stack([q4 ^ k for k in range(4)])

        m = wo.shape[0] // 2
        w2, w4 = swap(wo, xs), swap(wo, ys)
        w6a, w6b = swap(w2[:m], ys), swap(w4[m:], xs)
        ws = [wo, w2, w4, w6a, w6b]
        wp = [swap(w, core) for w in ws]
        wall = [ws[0], wp[0], ws[1], wp[1], ws[2], wp[2], ws[3], ws[4], wp[3], wp[4]]

        wk_l = lax.dynamic_slice_in_dim(wk, r * HEAD, HEAD, axis=1)
        wv_l = lax.dynamic_slice_in_dim(wv, r * HEAD, HEAD, axis=1)
        cos, sin = _cs(pos)
        q, k, v = _qkv(x, g1, jnp.concatenate([wq, wk_l, wv_l], axis=1), cos, sin, hl)
        kt = k.T

        y = None
        for n, rows in enumerate(chunks):
            half, piece = rows // 2, rows // 8
            o = _attn(q, kt, v, hl, q0s[n], rows)
            oa = lax.dynamic_slice_in_dim(o, c * half, half, axis=0)
            ob = swap(lax.dynamic_slice_in_dim(o, (1 - c) * half, half, axis=0), core)
            oax, oay = swap(oa, xs), swap(oa, ys)
            obx, oby = swap(ob, xs), swap(ob, ys)
            oad, obd = swap(oax, ys), swap(oby, xs)
            h, b = _h(q0s[n] + c * half, x, g2, [oa, ob, oax, obx, oay, oby, oad, obd], wall)
            p0 = _mlp(b, wg, wu, wd)
            p1 = _mlp(swap(b, core), wg, wu, wd)
            p1 = swap(p1, core)

            one, two = (1, 2) if n % 2 == 0 else (2, 1)
            via = {1: xs, 2: ys}
            f, g1st = _sums(qs, piece, [[(p0, 3), (p1, 3)], [(p0, one), (p1, one)]])
            f, g1st = swap(f, via[one]), swap(g1st, via[one])
            g2nd, = _sums(qs, piece, [[(p0, two), (p1, two), (f, None)]])
            g2nd = swap(g2nd, via[two])
            own, = _sums(qs, piece,
                          [[(p0, 0), (p1, 0), (g1st, None), (g2nd, None), (h, 0)]])
            got1, got2 = swap(own, via[one]), swap(own, via[two])
            got3 = swap(got1, via[two])
            mine = [own, got1, got2, got3]
            pieces = mine + [swap(s, core) for s in mine]
            at = jnp.stack([q0s[n] + cc * half + (q4 ^ kk) * piece for cc in (c, 1 - c) for kk in (0, one, two, 3)])
            y = _place(y, at, pieces, t)
        return y, k.reshape(t, 1, HEAD), v.reshape(t, 1, HEAD)

    return jax.shard_map(
        layer,
        mesh=mesh,
        in_specs=(P("dp", None), P("dp"), P(), P(), P(None, "tp"), P(), P(), P("tp", None),
                  P(None, "tp"), P(None, "tp"), P("tp", None)),
        out_specs=(P("dp", None), P("dp", "tp", None), P("dp", "tp", None)),
        check_vma=False,
    )
```

profile of v0, /device:TPU:0, one launch (start us, length us, event | category | flops | bytes accessed | tf_op | source)
XLA Modules:
  0.0 1396.3 jit_solution(1389015553613870777)
XLA Ops:
  2.7 17.9 %multiply_sine_fusion = (f32[8192,64]{1,0:T(8,128)}, f32[8192,64]{1,0:T(8,128)}) fusion(f32[64]{0:T(128)S(1)} %multiply_power_fusion, f32[8192]{0:T(1024)S(1)} %convert_element_type.3), kind=kLoop, calls=%fused_computation | loop fusion | flops 524288 | bytes 4227328 | tf_op jit(solution)/shard_map/sin | solution.py:24
  25.0 57.9 %qkv.1 = (bf16[8192,384]{1,0:T(8,128)(2,1)}, bf16[8192,128]{1,0:T(8,128)(2,1)}, bf16[8192,128]{1,0:T(8,128)(2,1)}) custom-call(bf16[8192,3072]{1,0:T(8,128)(2,1)} %x_ref.11, bf16[1,3072]{1,0:T(2,128)(2,1)} %reshape.45.g_ref, bf16[3072,640]{1,0:T(8,128)(2,1)} %pad_maximum_fusion.w_ref, f32[8192,64]{1,0:T(8,128)} %get-tuple-element.60.c_ref, ...), custom_call_target="tpu_custom_call" | custom-call | flops 32212254720 | bytes 50331648 | tf_op jit(solution)/shard_map/qkv/pallas_call | solution.py:51
  82.9 4.1 copy.18
  87.0 42.5 %shard_map.130 = bf16[1024,384]{1,0:T(8,128)(2,1)} custom-call(bf16[8192,384]{1,0:T(8,128)(2,1)} %get-tuple-element.26.q_ref, bf16[128,8192]{1,0:T(8,128)(2,1)} %bitcast.53, bf16[8192,128]{1,0:T(8,128)(2,1)} %get-tuple-element.28.v_ref), custom_call_target="tpu_custom_call" | custom-call | flops 37446746112 | bytes 4194304 | tf_op jit(solution)/shard_map/pallas_call | solution.py:133
  136.1 26.6 %shard_map.151 = bf16[1536,384]{1,0:T(8,128)(2,1)} custom-call(bf16[8192,384]{1,0:T(8,128)(2,1)} %get-tuple-element.26.q_ref, bf16[128,8192]{1,0:T(8,128)(2,1)} %bitcast.54, bf16[8192,128]{1,0:T(8,128)(2,1)} %get-tuple-element.28.v_ref), custom_call_target="tpu_custom_call" | custom-call | flops 21743271936 | bytes 1835008 | tf_op jit(solution)/shard_map/pallas_call | solution.py:133
  165.4 53.1 %shard_map.137 = bf16[1536,384]{1,0:T(8,128)(2,1)} custom-call(bf16[8192,384]{1,0:T(8,128)(2,1)} %get-tuple-element.26.q_ref, bf16[128,8192]{1,0:T(8,128)(2,1)} %bitcast.55, bf16[8192,128]{1,0:T(8,128)(2,1)} %get-tuple-element.28.v_ref), custom_call_target="tpu_custom_call" | custom-call | flops 47110422528 | bytes 3670016 | tf_op jit(solution)/shard_map/pallas_call | solution.py:133
  224.2 17.0 %shard_map.158 = bf16[2048,384]{1,0:T(8,128)(2,1)} custom-call(bf16[8192,384]{1,0:T(8,128)(2,1)} %get-tuple-element.26.q_ref, bf16[128,8192]{1,0:T(8,128)(2,1)} %bitcast.56, bf16[8192,128]{1,0:T(8,128)(2,1)} %get-tuple-element.28.v_ref), custom_call_target="tpu_custom_call" | custom-call | flops 12079595520 | bytes 1048576 | tf_op jit(solution)/shard_map/pallas_call | solution.py:133
  243.2 41.4 %collective-permute-done.69.refs_4_ = bf16[768,384]{1,0:T(8,128)(2,1)} collective-permute-done((bf16[768,384]{1,0:T(8,128)(2,1)S(1)}, bf16[768,384]{1,0:T(8,128)(2,1)}, u32[]{:S(2)}, u32[]{:S(2)}) %collective-permute-start.69) | collective-permute-done | bytes 589856 | tf_op jit(solution)/shard_map/ppermute | solution.py:343
  286.6 14.2 %collective-permute-done.29.refs_2_ = bf16[768,384]{1,0:T(8,128)(2,1)S(1)} collective-permute-done((bf16[768,384]{1,0:T(8,128)(2,1)S(1)}, bf16[768,384]{1,0:T(8,128)(2,1)S(1)}, u32[]{:S(2)}, u32[]{:S(2)}) %collective-permute-start.29) | collective-permute-done | bytes 589856 | tf_op jit(solution)/shard_map/ppermute | solution.py:343
  307.6 9.4 collective-permute-done.31.refs_4_
  319.0 14.8 %collective-permute-done.88.refs_4_ = bf16[1024,384]{1,0:T(8,128)(2,1)S(1)} collective-permute-done((bf16[1024,384]{1,0:T(8,128)(2,1)S(1)}, bf16[1024,384]{1,0:T(8,128)(2,1)S(1)}, u32[]{:S(2)}, u32[]{:S(2)}) %collective-permute-start.88) | collective-permute-done | bytes 786464 | tf_op jit(solution)/shard_map/ppermute | solution.py:343
  335.3 28.1 %collective-permute-done.70.refs_5_ = bf16[768,384]{1,0:T(8,128)(2,1)} collective-permute-done((bf16[768,384]{1,0:T(8,128)(2,1)}, bf16[768,384]{1,0:T(8,128)(2,1)}, u32[]{:S(2)}, u32[]{:S(2)}) %collective-permute-start.70) | collective-permute-done | bytes 589856 | tf_op jit(solution)/shard_map/ppermute | solution.py:343
  365.5 35.5 %collective-permute-done.90.refs_6_ = bf16[1024,384]{1,0:T(8,128)(2,1)S(1)} collective-permute-done((bf16[1024,384]{1,0:T(8,128)(2,1)S(1)}, bf16[1024,384]{1,0:T(8,128)(2,1)S(1)}, u32[]{:S(2)}, u32[]{:S(2)}) %collective-permute-start.90) | collective-permute-done | bytes 786464 | tf_op jit(solution)/shard_map/ppermute | solution.py:343
  402.4 52.0 %shard_map.144 = bf16[2048,384]{1,0:T(8,128)(2,1)} custom-call(bf16[8192,384]{1,0:T(8,128)(2,1)} %get-tuple-element.26.q_ref, bf16[128,8192]{1,0:T(8,128)(2,1)} %bitcast.57, bf16[8192,128]{1,0:T(8,128)(2,1)} %get-tuple-element.28.v_ref), custom_call_target="tpu_custom_call" | custom-call | flops 45902462976 | bytes 2883584 | tf_op jit(solution)/shard_map/pallas_call | solution.py:133
  462.3 32.3 %shard_map.159 = (bf16[1024,3072]{1,0:T(8,128)(2,1)}, bf16[1024,3072]{1,0:T(8,128)(2,1)}) custom-call(s32[1]{0:T(128)} %bitcast.49.off_ref, bf16[8192,3072]{1,0:T(8,128)(2,1)} %x_ref.11, bf16[1,3072]{1,0:T(2,128)(2,1)} %reshape.44.g_ref, bf16[1024,384]{1,0:T(8,128)(2,1)} %copy-done.5, bf16[1024,384]{1,0:T(8,128)(2,1)} %copy-done.21, ...), custom_call_target="tpu_custom_call" | custom-call | flops 19327352832 | bytes 44040192 | tf_op jit(solution)/shard_map/pallas_call | solution.py:181
  500.2 26.5 %shard_map.152 = (bf16[768,3072]{1,0:T(8,128)(2,1)}, bf16[768,3072]{1,0:T(8,128)(2,1)}) custom-call(s32[1]{0:T(128)} %bitcast.40.off_ref, bf16[8192,3072]{1,0:T(8,128)(2,1)} %x_ref.11, bf16[1,3072]{1,0:T(2,128)(2,1)} %reshape.44.g_ref, bf16[768,384]{1,0:T(8,128)(2,1)} %copy-done.9, bf16[768,384]{1,0:T(8,128)(2,1)} %collective-permute-done.66.refs_1_, ...), custom_call_target="tpu_custom_call" | custom-call | flops 14495514624 | bytes 37748736 | tf_op jit(solution)/shard_map/pallas_call | solution.py:181
  533.5 21.4 %shard_map.131 = (bf16[512,3072]{1,0:T(8,128)(2,1)}, bf16[512,3072]{1,0:T(8,128)(2,1)}) custom-call(s32[1]{0:T(128)} %bitcast.12.off_ref, bf16[8192,3072]{1,0:T(8,128)(2,1)} %x_ref.11, bf16[1,3072]{1,0:T(2,128)(2,1)} %reshape.44.g_ref, bf16[512,384]{1,0:T(8,128)(2,1)} %copy-done.10, bf16[512,384]{1,0:T(8,128)(2,1)} %collective-permute-done.refs_1_, ...), custom_call_target="tpu_custom_call" | custom-call | flops 9663676416 | bytes 31457280 | tf_op jit(solution)/shard_map/pallas_call | solution.py:181
  556.3 20.5 %collective-permute-done.51.refs_5_ = bf16[1024,384]{1,0:T(8,128)(2,1)} collective-permute-done((bf16[1024,384]{1,0:T(8,128)(2,1)}, bf16[1024,384]{1,0:T(8,128)(2,1)}, u32[]{:S(2)}, u32[]{:S(2)}) %collective-permute-start.51) | collective-permute-done | bytes 786464 | tf_op jit(solution)/shard_map/ppermute | solution.py:343
  577.9 26.5 %shard_map.138 = (bf16[768,3072]{1,0:T(8,128)(2,1)}, bf16[768,3072]{1,0:T(8,128)(2,1)}) custom-call(s32[1]{0:T(128)} %bitcast.22.off_ref, bf16[8192,3072]{1,0:T(8,128)(2,1)} %x_ref.11, bf16[1,3072]{1,0:T(2,128)(2,1)} %reshape.44.g_ref, bf16[768,384]{1,0:T(8,128)(2,1)} %copy-done.8, bf16[768,384]{1,0:T(8,128)(2,1)} %copy-done.32, ...), custom_call_target="tpu_custom_call" | custom-call | flops 14495514624 | bytes 37748736 | tf_op jit(solution)/shard_map/pallas_call | solution.py:181
  605.3 32.2 %shard_map.145 = (bf16[1024,3072]{1,0:T(8,128)(2,1)}, bf16[1024,3072]{1,0:T(8,128)(2,1)}) custom-call(s32[1]{0:T(128)} %bitcast.31.off_ref, bf16[8192,3072]{1,0:T(8,128)(2,1)} %x_ref.11, bf16[1,3072]{1,0:T(2,128)(2,1)} %reshape.44.g_ref, bf16[1024,384]{1,0:T(8,128)(2,1)} %copy-done.6, bf16[1024,384]{1,0:T(8,128)(2,1)} %collective-permute-done.47.refs_1_, ...), custom_call_target="tpu_custom_call" | custom-call | flops 19327352832 | bytes 44040192 | tf_op jit(solution)/shard_map/pallas_call | solution.py:181
  637.6 16.6 %shard_map.132.refs_0_.refs_2_ = bf16[512,3072]{1,0:T(8,128)(2,1)} custom-call(bf16[512,3072]{1,0:T(8,128)(2,1)} %get-tuple-element.29.b_ref, bf16[3072,1024]{1,0:T(8,128)(2,1)} %wg_ref.19, bf16[3072,1024]{1,0:T(8,128)(2,1)} %wu_ref.19, bf16[1024,3072]{1,0:T(8,128)(2,1)} %wd_ref.19), custom_call_target="tpu_custom_call" | custom-call | flops 9663676416 | bytes 25165824 | tf_op jit(solution)/shard_map/pallas_call | solution.py:250
  654.2 17.1 %shard_map.133 = bf16[512,3072]{1,0:T(8,128)(2,1)} custom-call(bf16[512,3072]{1,0:T(8,128)(2,1)} %collective-permute-done.16.b_ref, bf16[3072,1024]{1,0:T(8,128)(2,1)} %wg_ref.19, bf16[3072,1024]{1,0:T(8,128)(2,1)} %wu_ref.19, bf16[1024,3072]{1,0:T(8,128)(2,1)} %wd_ref.19), custom_call_target="tpu_custom_call" | custom-call | flops 9663676416 | bytes 25165824 | tf_op jit(solution)/shard_map/pallas_call | solution.py:250
  671.8 22.0 %shard_map.154 = bf16[768,3072]{1,0:T(8,128)(2,1)} custom-call(bf16[768,3072]{1,0:T(8,128)(2,1)} %collective-permute-done.73.b_ref, bf16[3072,1024]{1,0:T(8,128)(2,1)} %wg_ref.19, bf16[3072,1024]{1,0:T(8,128)(2,1)} %wu_ref.19, bf16[1024,3072]{1,0:T(8,128)(2,1)} %wd_ref.19), custom_call_target="tpu_custom_call" | custom-call | flops 14495514624 | bytes 28311552 | tf_op jit(solution)/shard_map/pallas_call | solution.py:250
  693.9 22.3 %shard_map.140 = bf16[768,3072]{1,0:T(8,128)(2,1)} custom-call(bf16[768,3072]{1,0:T(8,128)(2,1)} %collective-permute-done.35.b_ref, bf16[3072,1024]{1,0:T(8,128)(2,1)} %wg_ref.19, bf16[3072,1024]{1,0:T(8,128)(2,1)} %wu_ref.19, bf16[1024,3072]{1,0:T(8,128)(2,1)} %wd_ref.19), custom_call_target="tpu_custom_call" | custom-call | flops 14495514624 | bytes 28311552 | tf_op jit(solution)/shard_map/pallas_call | solution.py:250
  716.7 22.2 %shard_map.153.refs_0_.refs_2_ = bf16[768,3072]{1,0:T(8,128)(2,1)} custom-call(bf16[768,3072]{1,0:T(8,128)(2,1)} %get-tuple-element.41.b_ref, bf16[3072,1024]{1,0:T(8,128)(2,1)} %wg_ref.19, bf16[3072,1024]{1,0:T(8,128)(2,1)} %wu_ref.19, bf16[1024,3072]{1,0:T(8,128)(2,1)} %wd_ref.19), custom_call_target="tpu_custom_call" | custom-call | flops 14495514624 | bytes 28311552 | tf_op jit(solution)/shard_map/pallas_call | solution.py:250
  738.8 22.5 %shard_map.139.refs_0_.refs_2_ = bf16[768,3072]{1,0:T(8,128)(2,1)} custom-call(bf16[768,3072]{1,0:T(8,128)(2,1)} %get-tuple-element.33.b_ref, bf16[3072,1024]{1,0:T(8,128)(2,1)} %wg_ref.19, bf16[3072,1024]{1,0:T(8,128)(2,1)} %wu_ref.19, bf16[1024,3072]{1,0:T(8,128)(2,1)} %wd_ref.19), custom_call_target="tpu_custom_call" | custom-call | flops 14495514624 | bytes 28311552 | tf_op jit(solution)/shard_map/pallas_call | solution.py:250
  761.3 3.5 shard_map.134
  766.4 27.6 %shard_map.161 = bf16[1024,3072]{1,0:T(8,128)(2,1)} custom-call(bf16[1024,3072]{1,0:T(8,128)(2,1)} %collective-permute-done.92.b_ref, bf16[3072,1024]{1,0:T(8,128)(2,1)} %wg_ref.19, bf16[3072,1024]{1,0:T(8,128)(2,1)} %wu_ref.19, bf16[1024,3072]{1,0:T(8,128)(2,1)} %wd_ref.19), custom_call_target="tpu_custom_call" | custom-call | flops 19327352832 | bytes 31457280 | tf_op jit(solution)/shard_map/pallas_call | solution.py:250
  798.7 5.2 shard_map.155
  805.4 5.2 shard_map.141
  811.1 27.7 %shard_map.147 = bf16[1024,3072]{1,0:T(8,128)(2,1)} custom-call(bf16[1024,3072]{1,0:T(8,128)(2,1)} %collective-permute-done.54.b_ref, bf16[3072,1024]{1,0:T(8,128)(2,1)} %wg_ref.19, bf16[3072,1024]{1,0:T(8,128)(2,1)} %wu_ref.19, bf16[1024,3072]{1,0:T(8,128)(2,1)} %wd_ref.19), custom_call_target="tpu_custom_call" | custom-call | flops 19327352832 | bytes 31457280 | tf_op jit(solution)/shard_map/pallas_call | solution.py:250
  839.7 3.8 shard_map.136.refs_0_
  846.1 4.5 shard_map.156
  850.6 12.1 collective-permute-done.21.refs_1_
  865.2 4.3 collective-permute-done.38.refs_2_
  870.6 4.5 shard_map.142
  875.1 19.6 %collective-permute-done.75.refs_2_ = bf16[192,3072]{1,0:T(8,128)(2,1)} collective-permute-done((bf16[192,3072]{1,0:T(8,128)(2,1)}, bf16[192,3072]{1,0:T(8,128)(2,1)}, u32[]{:S(2)}, u32[]{:S(2)}) %collective-permute-start.75) | collective-permute-done | bytes 1179680 | tf_op jit(solution)/shard_map/ppermute | solution.py:343
  895.2 24.6 %collective-permute-done.37.refs_2_ = bf16[192,3072]{1,0:T(8,128)(2,1)S(1)} collective-permute-done((bf16[192,3072]{1,0:T(8,128)(2,1)}, bf16[192,3072]{1,0:T(8,128)(2,1)S(1)}, u32[]{:S(2)}, u32[]{:S(2)}) %collective-permute-start.37) | collective-permute-done | bytes 1179680 | tf_op jit(solution)/shard_map/ppermute | solution.py:343
  921.6 27.7 %shard_map.160.refs_0_.refs_2_ = bf16[1024,3072]{1,0:T(8,128)(2,1)} custom-call(bf16[1024,3072]{1,0:T(8,128)(2,1)} %get-tuple-element.45.b_ref, bf16[3072,1024]{1,0:T(8,128)(2,1)} %wg_ref.19, bf16[3072,1024]{1,0:T(8,128)(2,1)} %wu_ref.19, bf16[1024,3072]{1,0:T(8,128)(2,1)} %wd_ref.19), custom_call_target="tpu_custom_call" | custom-call | flops 19327352832 | bytes 31457280 | tf_op jit(solution)/shard_map/pallas_call | solution.py:250
  949.3 5.3 shard_map.157.refs_0_
  956.1 5.2 shard_map.143.refs_0_
  962.7 27.8 %shard_map.146.refs_0_.refs_2_ = bf16[1024,3072]{1,0:T(8,128)(2,1)} custom-call(bf16[1024,3072]{1,0:T(8,128)(2,1)} %get-tuple-element.37.b_ref, bf16[3072,1024]{1,0:T(8,128)(2,1)} %wg_ref.19, bf16[3072,1024]{1,0:T(8,128)(2,1)} %wu_ref.19, bf16[1024,3072]{1,0:T(8,128)(2,1)} %wd_ref.19), custom_call_target="tpu_custom_call" | custom-call | flops 19327352832 | bytes 31457280 | tf_op jit(solution)/shard_map/pallas_call | solution.py:250
  990.5 5.6 shard_map.162
  997.3 5.6 shard_map.148
  1006.0 27.7 %collective-permute-done.95.refs_2_ = bf16[256,3072]{1,0:T(8,128)(2,1)} collective-permute-done((bf16[256,3072]{1,0:T(8,128)(2,1)}, bf16[256,3072]{1,0:T(8,128)(2,1)}, u32[]{:S(2)}, u32[]{:S(2)}) %collective-permute-start.95) | collective-permute-done | bytes 1572896 | tf_op jit(solution)/shard_map/ppermute | solution.py:343
  1034.9 5.0 shard_map.163
  1039.9 27.5 %collective-permute-done.57.refs_2_ = bf16[256,3072]{1,0:T(8,128)(2,1)} collective-permute-done((bf16[256,3072]{1,0:T(8,128)(2,1)}, bf16[256,3072]{1,0:T(8,128)(2,1)}, u32[]{:S(2)}, u32[]{:S(2)}) %collective-permute-start.57) | collective-permute-done | bytes 1572896 | tf_op jit(solution)/shard_map/ppermute | solution.py:343
  1068.9 5.0 shard_map.149
  1074.0 52.5 %collective-permute-done.41.refs_2_ = bf16[192,3072]{1,0:T(8,128)(2,1)} collective-permute-done((bf16[192,3072]{1,0:T(8,128)(2,1)S(1)}, bf16[192,3072]{1,0:T(8,128)(2,1)}, u32[]{:S(2)}, u32[]{:S(2)}) %collective-permute-start.41) | collective-permute-done | bytes 1179680 | tf_op jit(solution)/shard_map/ppermute | solution.py:343
  1129.1 31.0 %collective-permute-done.56.refs_2_ = bf16[256,3072]{1,0:T(8,128)(2,1)} collective-permute-done((bf16[256,3072]{1,0:T(8,128)(2,1)}, bf16[256,3072]{1,0:T(8,128)(2,1)}, u32[]{:S(2)}, u32[]{:S(2)}) %collective-permute-start.56) | collective-permute-done | bytes 1572896 | tf_op jit(solution)/shard_map/ppermute | solution.py:343
  1160.1 24.5 %collective-permute-done.80.refs_3_ = bf16[192,3072]{1,0:T(8,128)(2,1)} collective-permute-done((bf16[192,3072]{1,0:T(8,128)(2,1)}, bf16[192,3072]{1,0:T(8,128)(2,1)}, u32[]{:S(2)}, u32[]{:S(2)}) %collective-permute-start.80) | collective-permute-done | bytes 1179680 | tf_op jit(solution)/shard_map/ppermute | solution.py:343
  1185.8 5.9 shard_map.164.refs_0_
  1192.8 6.0 shard_map.150.refs_0_
  1200.4 13.5 collective-permute-done.42.refs_3_
  1215.2 32.3 %collective-permute-done.97.refs_1_ = bf16[256,3072]{1,0:T(8,128)(2,1)} collective-permute-done((bf16[256,3072]{1,0:T(8,128)(2,1)}, bf16[256,3072]{1,0:T(8,128)(2,1)}, u32[]{:S(2)}, u32[]{:S(2)}) %collective-permute-start.97) | collective-permute-done | bytes 1572896 | tf_op jit(solution)/shard_map/ppermute | solution.py:343
  1251.2 28.4 %collective-permute-done.59.refs_1_ = bf16[256,3072]{1,0:T(8,128)(2,1)} collective-permute-done((bf16[256,3072]{1,0:T(8,128)(2,1)}, bf16[256,3072]{1,0:T(8,128)(2,1)}, u32[]{:S(2)}, u32[]{:S(2)}) %collective-permute-start.59) | collective-permute-done | bytes 1572896 | tf_op jit(solution)/shard_map/ppermute | solution.py:343
  1281.1 4.0 collective-permute-done.99.refs_3_
  1285.1 33.7 %collective-permute-done.60.refs_2_ = bf16[256,3072]{1,0:T(8,128)(2,1)} collective-permute-done((bf16[256,3072]{1,0:T(8,128)(2,1)}, bf16[256,3072]{1,0:T(8,128)(2,1)}, u32[]{:S(2)}, u32[]{:S(2)}) %collective-permute-start.60) | collective-permute-done | bytes 1572896 | tf_op jit(solution)/shard_map/ppermute | solution.py:343
  1320.0 28.4 %collective-permute-done.61.refs_3_ = bf16[256,3072]{1,0:T(8,128)(2,1)} collective-permute-done((bf16[256,3072]{1,0:T(8,128)(2,1)}, bf16[256,3072]{1,0:T(8,128)(2,1)}, u32[]{:S(2)}, u32[]{:S(2)}) %collective-permute-start.61) | collective-permute-done | bytes 1572896 | tf_op jit(solution)/shard_map/ppermute | solution.py:343
  1352.2 10.0 shard_map.165.refs_8_
  1362.3 8.1 shard_map.166.refs_8_
  1371.5 10.0 shard_map.167.refs_8_
  1381.5 8.0 shard_map.168.refs_8_
  1389.6 6.2 shard_map.169
  (282 shorter events, 110.4 us)
Async XLA Ops:
  130.7 90.0 %collective-permute-start.1 = (bf16[512,384]{1,0:T(8,128)(2,1)S(1)}, bf16[512,384]{1,0:T(8,128)(2,1)S(1)}, u32[]{:S(2)}, u32[]{:S(2)}) collective-permute-start(bf16[512,384]{1,0:T(8,128)(2,1)S(1)} %get-tuple-element.58.refs_0_), channel_id=1, source_target_pairs={{0,2},{1,3},{2,0},{3,1},{4,6},{5,7},{6,4},{7,5}} | collective-permute-start | bytes 1179656 | tf_op jit(solution)/shard_map/ppermute | solution.py:343
  134.0 88.6 %collective-permute-start.3 = (bf16[512,384]{1,0:T(8,128)(2,1)S(1)}, bf16[512,384]{1,0:T(8,128)(2,1)}, u32[]{:S(2)}, u32[]{:S(2)}) collective-permute-start(bf16[512,384]{1,0:T(8,128)(2,1)S(1)} %get-tuple-element.58.refs_0_), channel_id=1, source_target_pairs={{0,4},{1,5},{2,6},{3,7},{4,0},{5,1},{6,2},{7,3}} | collective-permute-start | bytes 1179656 | tf_op jit(solution)/shard_map/ppermute | solution.py:343
  135.6 167.3 %collective-permute-start.8 = (bf16[384,3072]{1,0:T(8,128)(2,1)}, bf16[384,3072]{1,0:T(8,128)(2,1)}, u32[]{:S(2)}, u32[]{:S(2)}) collective-permute-start(bf16[384,3072]{1,0:T(8,128)(2,1)} %refs_8_.9), channel_id=1, source_target_pairs={{0,2},{1,3},{2,0},{3,1},{4,6},{5,7},{6,4},{7,5}} | collective-permute-start | bytes 7077896 | tf_op jit(solution)/shard_map/ppermute | solution.py:343
  164.9 59.3 %collective-permute-start.66 = (bf16[768,384]{1,0:T(8,128)(2,1)}, bf16[768,384]{1,0:T(8,128)(2,1)}, u32[]{:S(2)}, u32[]{:S(2)}) collective-permute-start(bf16[768,384]{1,0:T(8,128)(2,1)} %get-tuple-element.53), channel_id=1, source_target_pairs={{0,1},{1,0},{2,3},{3,2},{4,5},{5,4},{6,7},{7,6}} | collective-permute-start | bytes 1769480 | tf_op jit(solution)/shard_map/ppermute | solution.py:343
  164.9 53.6 %collective-permute-start = (bf16[512,384]{1,0:T(8,128)(2,1)S(1)}, bf16[512,384]{1,0:T(8,128)(2,1)}, u32[]{:S(2)}, u32[]{:S(2)}) collective-permute-start(bf16[512,384]{1,0:T(8,128)(2,1)S(1)} %get-tuple-element.57), channel_id=1, source_target_pairs={{0,1},{1,0},{2,3},{3,2},{4,5},{5,4},{6,7},{7,6}} | collective-permute-start | bytes 1179656 | tf_op jit(solution)/shard_map/ppermute | solution.py:343
  218.5 84.6 %collective-permute-start.10 = (bf16[384,3072]{1,0:T(8,128)(2,1)}, bf16[384,3072]{1,0:T(8,128)(2,1)}, u32[]{:S(2)}, u32[]{:S(2)}) collective-permute-start(bf16[384,3072]{1,0:T(8,128)(2,1)} %refs_8_.9), channel_id=1, source_target_pairs={{0,4},{1,5},{2,6},{3,7},{4,0},{5,1},{6,2},{7,3}} | collective-permute-start | bytes 7077896 | tf_op jit(solution)/shard_map/ppermute | solution.py:343
  222.7 61.9 %collective-permute-start.69 = (bf16[768,384]{1,0:T(8,128)(2,1)S(1)}, bf16[768,384]{1,0:T(8,128)(2,1)}, u32[]{:S(2)}, u32[]{:S(2)}) collective-permute-start(bf16[768,384]{1,0:T(8,128)(2,1)S(1)} %get-tuple-element.54.refs_0_), channel_id=1, source_target_pairs={{0,4},{1,5},{2,6},{3,7},{4,0},{5,1},{6,2},{7,3}} | collective-permute-start | bytes 1769480 | tf_op jit(solution)/shard_map/ppermute | solution.py:343
  224.2 61.9 %collective-permute-start.28 = (bf16[768,384]{1,0:T(8,128)(2,1)}, bf16[768,384]{1,0:T(8,128)(2,1)S(1)}, u32[]{:S(2)}, u32[]{:S(2)}) collective-permute-start(bf16[768,384]{1,0:T(8,128)(2,1)} %get-tuple-element.55), channel_id=1, source_target_pairs={{0,1},{1,0},{2,3},{3,2},{4,5},{5,4},{6,7},{7,6}} | collective-permute-start | bytes 1769480 | tf_op jit(solution)/shard_map/ppermute | solution.py:343
  242.7 58.4 %collective-permute-start.85 = (bf16[1024,384]{1,0:T(8,128)(2,1)S(1)}, bf16[1024,384]{1,0:T(8,128)(2,1)S(1)}, u32[]{:S(2)}, u32[]{:S(2)}) collective-permute-start(bf16[1024,384]{1,0:T(8,128)(2,1)S(1)} %get-tuple-element.49), channel_id=1, source_target_pairs={{0,1},{1,0},{2,3},{3,2},{4,5},{5,4},{6,7},{7,6}} | collective-permute-start | bytes 2359304 | tf_op jit(solution)/shard_map/ppermute | solution.py:343
  302.8 60.9 %collective-permute-start.89 = (bf16[1024,384]{1,0:T(8,128)(2,1)S(1)}, bf16[1024,384]{1,0:T(8,128)(2,1)S(1)}, u32[]{:S(2)}, u32[]{:S(2)}) collective-permute-start(bf16[1024,384]{1,0:T(8,128)(2,1)S(1)} %collective-permute-done.85.refs_1_), channel_id=1, source_target_pairs={{0,4},{1,5},{2,6},{3,7},{4,0},{5,1},{6,2},{7,3}} | collective-permute-start | bytes 2359304 | tf_op jit(solution)/shard_map/ppermute | solution.py:343
  303.1 60.3 %collective-permute-start.70 = (bf16[768,384]{1,0:T(8,128)(2,1)}, bf16[768,384]{1,0:T(8,128)(2,1)}, u32[]{:S(2)}, u32[]{:S(2)}) collective-permute-start(bf16[768,384]{1,0:T(8,128)(2,1)} %collective-permute-done.66.refs_1_), channel_id=1, source_target_pairs={{0,4},{1,5},{2,6},{3,7},{4,0},{5,1},{6,2},{7,3}} | collective-permute-start | bytes 1769480 | tf_op jit(solution)/shard_map/ppermute | solution.py:343
  317.0 84.5 %collective-permute-start.12 = (bf16[192,3072]{1,0:T(8,128)(2,1)S(1)}, bf16[192,3072]{1,0:T(8,128)(2,1)S(1)}, u32[]{:S(2)}, u32[]{:S(2)}) collective-permute-start(bf16[192,3072]{1,0:T(8,128)(2,1)S(1)} %slice.8), channel_id=1, source_target_pairs={{0,4},{1,5},{2,6},{3,7},{4,0},{5,1},{6,2},{7,3}} | collective-permute-start | bytes 3538952 | tf_op jit(solution)/shard_map/ppermute | solution.py:343
  317.3 84.3 %collective-permute-start.13 = (bf16[192,3072]{1,0:T(8,128)(2,1)S(1)}, bf16[192,3072]{1,0:T(8,128)(2,1)}, u32[]{:S(2)}, u32[]{:S(2)}) collective-permute-start(bf16[192,3072]{1,0:T(8,128)(2,1)S(1)} %slice.9), channel_id=1, source_target_pairs={{0,2},{1,3},{2,0},{3,1},{4,6},{5,7},{6,4},{7,5}} | collective-permute-start | bytes 3538952 | tf_op jit(solution)/shard_map/ppermute | solution.py:343
  365.4 92.6 %collective-permute-start.7 = (bf16[384,3072]{1,0:T(8,128)(2,1)}, bf16[384,3072]{1,0:T(8,128)(2,1)}, u32[]{:S(2)}, u32[]{:S(2)}) collective-permute-start(bf16[384,3072]{1,0:T(8,128)(2,1)} %refs_8_.9), channel_id=1, source_target_pairs={{0,1},{1,0},{2,3},{3,2},{4,5},{5,4},{6,7},{7,6}} | collective-permute-start | bytes 7077896 | tf_op jit(solution)/shard_map/ppermute | solution.py:343
  401.0 59.3 %collective-permute-start.11 = (bf16[384,3072]{1,0:T(8,128)(2,1)}, bf16[384,3072]{1,0:T(8,128)(2,1)}, u32[]{:S(2)}, u32[]{:S(2)}) collective-permute-start(bf16[384,3072]{1,0:T(8,128)(2,1)} %collective-permute-done.10.refs_12_), channel_id=1, source_target_pairs={{0,1},{1,0},{2,3},{3,2},{4,5},{5,4},{6,7},{7,6}} | collective-permute-start | bytes 7077896 | tf_op jit(solution)/shard_map/ppermute | solution.py:343
  401.0 60.8 %collective-permute-start.9 = (bf16[384,3072]{1,0:T(8,128)(2,1)}, bf16[384,3072]{1,0:T(8,128)(2,1)}, u32[]{:S(2)}, u32[]{:S(2)}) collective-permute-start(bf16[384,3072]{1,0:T(8,128)(2,1)} %collective-permute-done.8.refs_10_), channel_id=1, source_target_pairs={{0,1},{1,0},{2,3},{3,2},{4,5},{5,4},{6,7},{7,6}} | collective-permute-start | bytes 7077896 | tf_op jit(solution)/shard_map/ppermute | solution.py:343
  401.5 56.8 %collective-permute-start.14 = (bf16[192,3072]{1,0:T(8,128)(2,1)S(1)}, bf16[192,3072]{1,0:T(8,128)(2,1)}, u32[]{:S(2)}, u32[]{:S(2)}) collective-permute-start(bf16[192,3072]{1,0:T(8,128)(2,1)S(1)} %collective-permute-done.12.refs_14_), channel_id=1, source_target_pairs={{0,1},{1,0},{2,3},{3,2},{4,5},{5,4},{6,7},{7,6}} | collective-permute-start | bytes 3538952 | tf_op jit(solution)/shard_map/ppermute | solution.py:343
  402.1 57.0 %collective-permute-start.15 = (bf16[192,3072]{1,0:T(8,128)(2,1)}, bf16[192,3072]{1,0:T(8,128)(2,1)}, u32[]{:S(2)}, u32[]{:S(2)}) collective-permute-start(bf16[192,3072]{1,0:T(8,128)(2,1)} %collective-permute-done.13.refs_15_), channel_id=1, source_target_pairs={{0,1},{1,0},{2,3},{3,2},{4,5},{5,4},{6,7},{7,6}} | collective-permute-start | bytes 3538952 | tf_op jit(solution)/shard_map/ppermute | solution.py:343
  528.2 49.2 %collective-permute-start.33 = (bf16[768,384]{1,0:T(8,128)(2,1)}, bf16[768,384]{1,0:T(8,128)(2,1)}, u32[]{:S(2)}, u32[]{:S(2)}) collective-permute-start(bf16[768,384]{1,0:T(8,128)(2,1)} %copy-done.33), channel_id=1, source_target_pairs={{0,4},{1,5},{2,6},{3,7},{4,0},{5,1},{6,2},{7,3}} | collective-permute-start | bytes 1769480 | tf_op jit(solution)/shard_map/ppermute | solution.py:343
  529.4 47.4 %collective-permute-start.51 = (bf16[1024,384]{1,0:T(8,128)(2,1)}, bf16[1024,384]{1,0:T(8,128)(2,1)}, u32[]{:S(2)}, u32[]{:S(2)}) collective-permute-start(bf16[1024,384]{1,0:T(8,128)(2,1)} %collective-permute-done.47.refs_1_), channel_id=1, source_target_pairs={{0,4},{1,5},{2,6},{3,7},{4,0},{5,1},{6,2},{7,3}} | collective-permute-start | bytes 2359304 | tf_op jit(solution)/shard_map/ppermute | solution.py:343
  532.0 45.3 %collective-permute-start.34 = (bf16[768,384]{1,0:T(8,128)(2,1)}, bf16[768,384]{1,0:T(8,128)(2,1)}, u32[]{:S(2)}, u32[]{:S(2)}) collective-permute-start(bf16[768,384]{1,0:T(8,128)(2,1)} %collective-permute-done.32.refs_5_), channel_id=1, source_target_pairs={{0,2},{1,3},{2,0},{3,1},{4,6},{5,7},{6,4},{7,5}} | collective-permute-start | bytes 1769480 | tf_op jit(solution)/shard_map/ppermute | solution.py:343
  554.9 49.5 %collective-permute-start.49 = (bf16[1024,384]{1,0:T(8,128)(2,1)}, bf16[1024,384]{1,0:T(8,128)(2,1)S(1)}, u32[]{:S(2)}, u32[]{:S(2)}) collective-permute-start(bf16[1024,384]{1,0:T(8,128)(2,1)} %collective-permute-done.47.refs_1_), channel_id=1, source_target_pairs={{0,2},{1,3},{2,0},{3,1},{4,6},{5,7},{6,4},{7,5}} | collective-permute-start | bytes 2359304 | tf_op jit(solution)/shard_map/ppermute | solution.py:343
  555.5 49.0 %collective-permute-start.52 = (bf16[1024,384]{1,0:T(8,128)(2,1)S(1)}, bf16[1024,384]{1,0:T(8,128)(2,1)}, u32[]{:S(2)}, u32[]{:S(2)}) collective-permute-start(bf16[1024,384]{1,0:T(8,128)(2,1)S(1)} %collective-permute-done.48.refs_2_), channel_id=1, source_target_pairs={{0,4},{1,5},{2,6},{3,7},{4,0},{5,1},{6,2},{7,3}} | collective-permute-start | bytes 2359304 | tf_op jit(solution)/shard_map/ppermute | solution.py:343
  577.3 94.5 %collective-permute-start.73 = (bf16[768,3072]{1,0:T(8,128)(2,1)}, bf16[768,3072]{1,0:T(8,128)(2,1)}, u32[]{:S(2)}, u32[]{:S(2)}) collective-permute-start(bf16[768,3072]{1,0:T(8,128)(2,1)} %get-tuple-element.41.b_ref), channel_id=1, source_target_pairs={{0,1},{1,0},{2,3},{3,2},{4,5},{5,4},{6,7},{7,6}} | collective-permute-start | bytes 14155784 | tf_op jit(solution)/shard_map/ppermute | solution.py:343
  577.4 76.9 %collective-permute-start.16 = (bf16[512,3072]{1,0:T(8,128)(2,1)}, bf16[512,3072]{1,0:T(8,128)(2,1)}, u32[]{:S(2)}, u32[]{:S(2)}) collective-permute-start(bf16[512,3072]{1,0:T(8,128)(2,1)} %get-tuple-element.29.b_ref), channel_id=1, source_target_pairs={{0,1},{1,0},{2,3},{3,2},{4,5},{5,4},{6,7},{7,6}} | collective-permute-start | bytes 9437192 | tf_op jit(solution)/shard_map/ppermute | solution.py:343
  604.4 162.0 %collective-permute-start.92 = (bf16[1024,3072]{1,0:T(8,128)(2,1)}, bf16[1024,3072]{1,0:T(8,128)(2,1)}, u32[]{:S(2)}, u32[]{:S(2)}) collective-permute-start(bf16[1024,3072]{1,0:T(8,128)(2,1)} %get-tuple-element.45.b_ref), channel_id=1, source_target_pairs={{0,1},{1,0},{2,3},{3,2},{4,5},{5,4},{6,7},{7,6}} | collective-permute-start | bytes 18874376 | tf_op jit(solution)/shard_map/ppermute | solution.py:343
  604.4 89.5 %collective-permute-start.35 = (bf16[768,3072]{1,0:T(8,128)(2,1)}, bf16[768,3072]{1,0:T(8,128)(2,1)}, u32[]{:S(2)}, u32[]{:S(2)}) collective-permute-start(bf16[768,3072]{1,0:T(8,128)(2,1)} %get-tuple-element.33.b_ref), channel_id=1, source_target_pairs={{0,1},{1,0},{2,3},{3,2},{4,5},{5,4},{6,7},{7,6}} | collective-permute-start | bytes 14155784 | tf_op jit(solution)/shard_map/ppermute | solution.py:343
  637.5 173.0 %collective-permute-start.54 = (bf16[1024,3072]{1,0:T(8,128)(2,1)}, bf16[1024,3072]{1,0:T(8,128)(2,1)}, u32[]{:S(2)}, u32[]{:S(2)}) collective-permute-start(bf16[1024,3072]{1,0:T(8,128)(2,1)} %get-tuple-element.37.b_ref), channel_id=1, source_target_pairs={{0,1},{1,0},{2,3},{3,2},{4,5},{5,4},{6,7},{7,6}} | collective-permute-start | bytes 18874376 | tf_op jit(solution)/shard_map/ppermute | solution.py:343
  671.3 90.0 %collective-permute-start.17 = (bf16[512,3072]{1,0:T(8,128)(2,1)}, bf16[512,3072]{1,0:T(8,128)(2,1)}, u32[]{:S(2)}, u32[]{:S(2)}) collective-permute-start(bf16[512,3072]{1,0:T(8,128)(2,1)} %shard_map.133), channel_id=1, source_target_pairs={{0,1},{1,0},{2,3},{3,2},{4,5},{5,4},{6,7},{7,6}} | collective-permute-start | bytes 9437192 | tf_op jit(solution)/shard_map/ppermute | solution.py:343
  693.8 104.3 %collective-permute-start.74 = (bf16[768,3072]{1,0:T(8,128)(2,1)}, bf16[768,3072]{1,0:T(8,128)(2,1)}, u32[]{:S(2)}, u32[]{:S(2)}) collective-permute-start(bf16[768,3072]{1,0:T(8,128)(2,1)} %shard_map.154), channel_id=1, source_target_pairs={{0,1},{1,0},{2,3},{3,2},{4,5},{5,4},{6,7},{7,6}} | collective-permute-start | bytes 14155784 | tf_op jit(solution)/shard_map/ppermute | solution.py:343
  716.2 87.7 %collective-permute-start.36 = (bf16[768,3072]{1,0:T(8,128)(2,1)}, bf16[768,3072]{1,0:T(8,128)(2,1)}, u32[]{:S(2)}, u32[]{:S(2)}) collective-permute-start(bf16[768,3072]{1,0:T(8,128)(2,1)} %shard_map.140), channel_id=1, source_target_pairs={{0,1},{1,0},{2,3},{3,2},{4,5},{5,4},{6,7},{7,6}} | collective-permute-start | bytes 14155784 | tf_op jit(solution)/shard_map/ppermute | solution.py:343
  794.0 168.1 %collective-permute-start.93 = (bf16[1024,3072]{1,0:T(8,128)(2,1)}, bf16[1024,3072]{1,0:T(8,128)(2,1)}, u32[]{:S(2)}, u32[]{:S(2)}) collective-permute-start(bf16[1024,3072]{1,0:T(8,128)(2,1)} %shard_map.161), channel_id=1, source_target_pairs={{0,1},{1,0},{2,3},{3,2},{4,5},{5,4},{6,7},{7,6}} | collective-permute-start | bytes 18874376 | tf_op jit(solution)/shard_map/ppermute | solution.py:343
  794.1 44.7 %collective-permute-start.18 = (bf16[128,3072]{1,0:T(8,128)(2,1)}, bf16[128,3072]{1,0:T(8,128)(2,1)S(1)}, u32[]{:S(2)}, u32[]{:S(2)}) collective-permute-start(bf16[128,3072]{1,0:T(8,128)(2,1)} %get-tuple-element.30), channel_id=1, source_target_pairs={{0,2},{1,3},{2,0},{3,1},{4,6},{5,7},{6,4},{7,5}} | collective-permute-start | bytes 2359304 | tf_op jit(solution)/shard_map/ppermute | solution.py:343
  810.6 58.9 %collective-permute-start.38 = (bf16[192,3072]{1,0:T(8,128)(2,1)}, bf16[192,3072]{1,0:T(8,128)(2,1)}, u32[]{:S(2)}, u32[]{:S(2)}) collective-permute-start(bf16[192,3072]{1,0:T(8,128)(2,1)} %get-tuple-element.35), channel_id=1, source_target_pairs={{0,4},{1,5},{2,6},{3,7},{4,0},{5,1},{6,2},{7,3}} | collective-permute-start | bytes 3538952 | tf_op jit(solution)/shard_map/ppermute | solution.py:343
  838.8 157.3 %collective-permute-start.55 = (bf16[1024,3072]{1,0:T(8,128)(2,1)}, bf16[1024,3072]{1,0:T(8,128)(2,1)}, u32[]{:S(2)}, u32[]{:S(2)}) collective-permute-start(bf16[1024,3072]{1,0:T(8,128)(2,1)} %shard_map.147), channel_id=1, source_target_pairs={{0,1},{1,0},{2,3},{3,2},{4,5},{5,4},{6,7},{7,6}} | collective-permute-start | bytes 18874376 | tf_op jit(solution)/shard_map/ppermute | solution.py:343
  844.6 50.1 %collective-permute-start.75 = (bf16[192,3072]{1,0:T(8,128)(2,1)}, bf16[192,3072]{1,0:T(8,128)(2,1)}, u32[]{:S(2)}, u32[]{:S(2)}) collective-permute-start(bf16[192,3072]{1,0:T(8,128)(2,1)} %get-tuple-element.42), channel_id=1, source_target_pairs={{0,4},{1,5},{2,6},{3,7},{4,0},{5,1},{6,2},{7,3}} | collective-permute-start | bytes 3538952 | tf_op jit(solution)/shard_map/ppermute | solution.py:343
  863.7 56.2 %collective-permute-start.37 = (bf16[192,3072]{1,0:T(8,128)(2,1)}, bf16[192,3072]{1,0:T(8,128)(2,1)S(1)}, u32[]{:S(2)}, u32[]{:S(2)}) collective-permute-start(bf16[192,3072]{1,0:T(8,128)(2,1)} %get-tuple-element.34), channel_id=1, source_target_pairs={{0,4},{1,5},{2,6},{3,7},{4,0},{5,1},{6,2},{7,3}} | collective-permute-start | bytes 3538952 | tf_op jit(solution)/shard_map/ppermute | solution.py:343
  869.4 51.0 %collective-permute-start.77 = (bf16[192,3072]{1,0:T(8,128)(2,1)}, bf16[192,3072]{1,0:T(8,128)(2,1)}, u32[]{:S(2)}, u32[]{:S(2)}) collective-permute-start(bf16[192,3072]{1,0:T(8,128)(2,1)} %shard_map.156), channel_id=1, source_target_pairs={{0,2},{1,3},{2,0},{3,1},{4,6},{5,7},{6,4},{7,5}} | collective-permute-start | bytes 3538952 | tf_op jit(solution)/shard_map/ppermute | solution.py:343
  894.7 66.6 %collective-permute-start.22 = (bf16[128,3072]{1,0:T(8,128)(2,1)S(1)}, bf16[128,3072]{1,0:T(8,128)(2,1)}, u32[]{:S(2)}, u32[]{:S(2)}) collective-permute-start(bf16[128,3072]{1,0:T(8,128)(2,1)S(1)} %copy-done.3), channel_id=1, source_target_pairs={{0,4},{1,5},{2,6},{3,7},{4,0},{5,1},{6,2},{7,3}} | collective-permute-start | bytes 2359304 | tf_op jit(solution)/shard_map/ppermute | solution.py:343
  919.9 42.3 %collective-permute-start.23 = (bf16[128,3072]{1,0:T(8,128)(2,1)}, bf16[128,3072]{1,0:T(8,128)(2,1)}, u32[]{:S(2)}, u32[]{:S(2)}) collective-permute-start(bf16[128,3072]{1,0:T(8,128)(2,1)} %copy-done.19), channel_id=1, source_target_pairs={{0,4},{1,5},{2,6},{3,7},{4,0},{5,1},{6,2},{7,3}} | collective-permute-start | bytes 2359304 | tf_op jit(solution)/shard_map/ppermute | solution.py:343
  954.5 48.4 %collective-permute-start.78 = (bf16[192,3072]{1,0:T(8,128)(2,1)}, bf16[192,3072]{1,0:T(8,128)(2,1)}, u32[]{:S(2)}, u32[]{:S(2)}) collective-permute-start(bf16[192,3072]{1,0:T(8,128)(2,1)} %shard_map.157.refs_0_), channel_id=1, source_target_pairs={{0,4},{1,5},{2,6},{3,7},{4,0},{5,1},{6,2},{7,3}} | collective-permute-start | bytes 3538952 | tf_op jit(solution)/shard_map/ppermute | solution.py:343
  961.3 42.5 %collective-permute-start.79 = (bf16[192,3072]{1,0:T(8,128)(2,1)}, bf16[192,3072]{1,0:T(8,128)(2,1)}, u32[]{:S(2)}, u32[]{:S(2)}) collective-permute-start(bf16[192,3072]{1,0:T(8,128)(2,1)} %shard_map.157.refs_0_), channel_id=1, source_target_pairs={{0,2},{1,3},{2,0},{3,1},{4,6},{5,7},{6,4},{7,5}} | collective-permute-start | bytes 3538952 | tf_op jit(solution)/shard_map/ppermute | solution.py:343
  962.2 42.8 %collective-permute-start.81 = (bf16[192,3072]{1,0:T(8,128)(2,1)}, bf16[192,3072]{1,0:T(8,128)(2,1)}, u32[]{:S(2)}, u32[]{:S(2)}) collective-permute-start(bf16[192,3072]{1,0:T(8,128)(2,1)} %shard_map.157.refs_0_), channel_id=1, source_target_pairs={{0,1},{1,0},{2,3},{3,2},{4,5},{5,4},{6,7},{7,6}} | collective-permute-start | bytes 3538952 | tf_op jit(solution)/shard_map/ppermute | solution.py:343
  962.2 43.9 %collective-permute-start.40 = (bf16[192,3072]{1,0:T(8,128)(2,1)}, bf16[192,3072]{1,0:T(8,128)(2,1)}, u32[]{:S(2)}, u32[]{:S(2)}) collective-permute-start(bf16[192,3072]{1,0:T(8,128)(2,1)} %shard_map.143.refs_0_), channel_id=1, source_target_pairs={{0,4},{1,5},{2,6},{3,7},{4,0},{5,1},{6,2},{7,3}} | collective-permute-start | bytes 3538952 | tf_op jit(solution)/shard_map/ppermute | solution.py:343
  1002.9 64.5 %collective-permute-start.57 = (bf16[256,3072]{1,0:T(8,128)(2,1)}, bf16[256,3072]{1,0:T(8,128)(2,1)}, u32[]{:S(2)}, u32[]{:S(2)}) collective-permute-start(bf16[256,3072]{1,0:T(8,128)(2,1)} %get-tuple-element.39), channel_id=1, source_target_pairs={{0,2},{1,3},{2,0},{3,1},{4,6},{5,7},{6,4},{7,5}} | collective-permute-start | bytes 4718600 | tf_op jit(solution)/shard_map/ppermute | solution.py:343
  1003.8 125.3 %collective-permute-start.94 = (bf16[256,3072]{1,0:T(8,128)(2,1)}, bf16[256,3072]{1,0:T(8,128)(2,1)}, u32[]{:S(2)}, u32[]{:S(2)}) collective-permute-start(bf16[256,3072]{1,0:T(8,128)(2,1)} %get-tuple-element.46), channel_id=1, source_target_pairs={{0,2},{1,3},{2,0},{3,1},{4,6},{5,7},{6,4},{7,5}} | collective-permute-start | bytes 4718600 | tf_op jit(solution)/shard_map/ppermute | solution.py:343
  1005.0 121.5 %collective-permute-start.41 = (bf16[192,3072]{1,0:T(8,128)(2,1)S(1)}, bf16[192,3072]{1,0:T(8,128)(2,1)}, u32[]{:S(2)}, u32[]{:S(2)}) collective-permute-start(bf16[192,3072]{1,0:T(8,128)(2,1)S(1)} %copy-done.2), channel_id=1, source_target_pairs={{0,2},{1,3},{2,0},{3,1},{4,6},{5,7},{6,4},{7,5}} | collective-permute-start | bytes 3538952 | tf_op jit(solution)/shard_map/ppermute | solution.py:343
  1006.0 121.9 %collective-permute-start.43 = (bf16[192,3072]{1,0:T(8,128)(2,1)S(1)}, bf16[192,3072]{1,0:T(8,128)(2,1)}, u32[]{:S(2)}, u32[]{:S(2)}) collective-permute-start(bf16[192,3072]{1,0:T(8,128)(2,1)S(1)} %copy-done.2), channel_id=1, source_target_pairs={{0,1},{1,0},{2,3},{3,2},{4,5},{5,4},{6,7},{7,6}} | collective-permute-start | bytes 3538952 | tf_op jit(solution)/shard_map/ppermute | solution.py:343
  1033.7 126.4 %collective-permute-start.56 = (bf16[256,3072]{1,0:T(8,128)(2,1)}, bf16[256,3072]{1,0:T(8,128)(2,1)}, u32[]{:S(2)}, u32[]{:S(2)}) collective-permute-start(bf16[256,3072]{1,0:T(8,128)(2,1)} %get-tuple-element.38), channel_id=1, source_target_pairs={{0,2},{1,3},{2,0},{3,1},{4,6},{5,7},{6,4},{7,5}} | collective-permute-start | bytes 4718600 | tf_op jit(solution)/shard_map/ppermute | solution.py:343
  1067.5 118.4 %collective-permute-start.96 = (bf16[256,3072]{1,0:T(8,128)(2,1)}, bf16[256,3072]{1,0:T(8,128)(2,1)}, u32[]{:S(2)}, u32[]{:S(2)}) collective-permute-start(bf16[256,3072]{1,0:T(8,128)(2,1)} %shard_map.163), channel_id=1, source_target_pairs={{0,4},{1,5},{2,6},{3,7},{4,0},{5,1},{6,2},{7,3}} | collective-permute-start | bytes 4718600 | tf_op jit(solution)/shard_map/ppermute | solution.py:343
  1126.4 66.2 %collective-permute-start.58 = (bf16[256,3072]{1,0:T(8,128)(2,1)}, bf16[256,3072]{1,0:T(8,128)(2,1)}, u32[]{:S(2)}, u32[]{:S(2)}) collective-permute-start(bf16[256,3072]{1,0:T(8,128)(2,1)} %shard_map.149), channel_id=1, source_target_pairs={{0,4},{1,5},{2,6},{3,7},{4,0},{5,1},{6,2},{7,3}} | collective-permute-start | bytes 4718600 | tf_op jit(solution)/shard_map/ppermute | solution.py:343
  1127.9 56.7 %collective-permute-start.80 = (bf16[192,3072]{1,0:T(8,128)(2,1)}, bf16[192,3072]{1,0:T(8,128)(2,1)}, u32[]{:S(2)}, u32[]{:S(2)}) collective-permute-start(bf16[192,3072]{1,0:T(8,128)(2,1)} %collective-permute-done.78.refs_1_), channel_id=1, source_target_pairs={{0,2},{1,3},{2,0},{3,1},{4,6},{5,7},{6,4},{7,5}} | collective-permute-start | bytes 3538952 | tf_op jit(solution)/shard_map/ppermute | solution.py:343
  1129.1 62.6 %collective-permute-start.82 = (bf16[192,3072]{1,0:T(8,128)(2,1)}, bf16[192,3072]{1,0:T(8,128)(2,1)S(1)}, u32[]{:S(2)}, u32[]{:S(2)}) collective-permute-start(bf16[192,3072]{1,0:T(8,128)(2,1)} %collective-permute-done.78.refs_1_), channel_id=1, source_target_pairs={{0,1},{1,0},{2,3},{3,2},{4,5},{5,4},{6,7},{7,6}} | collective-permute-start | bytes 3538952 | tf_op jit(solution)/shard_map/ppermute | solution.py:343
  1191.7 55.8 %collective-permute-start.97 = (bf16[256,3072]{1,0:T(8,128)(2,1)}, bf16[256,3072]{1,0:T(8,128)(2,1)}, u32[]{:S(2)}, u32[]{:S(2)}) collective-permute-start(bf16[256,3072]{1,0:T(8,128)(2,1)} %shard_map.164.refs_0_), channel_id=1, source_target_pairs={{0,2},{1,3},{2,0},{3,1},{4,6},{5,7},{6,4},{7,5}} | collective-permute-start | bytes 4718600 | tf_op jit(solution)/shard_map/ppermute | solution.py:343
  1198.8 51.2 %collective-permute-start.98 = (bf16[256,3072]{1,0:T(8,128)(2,1)S(1)}, bf16[256,3072]{1,0:T(8,128)(2,1)S(1)}, u32[]{:S(2)}, u32[]{:S(2)}) collective-permute-start(bf16[256,3072]{1,0:T(8,128)(2,1)S(1)} %copy-done.1), channel_id=1, source_target_pairs={{0,4},{1,5},{2,6},{3,7},{4,0},{5,1},{6,2},{7,3}} | collective-permute-start | bytes 4718600 | tf_op jit(solution)/shard_map/ppermute | solution.py:343
  1213.8 65.8 %collective-permute-start.59 = (bf16[256,3072]{1,0:T(8,128)(2,1)}, bf16[256,3072]{1,0:T(8,128)(2,1)}, u32[]{:S(2)}, u32[]{:S(2)}) collective-permute-start(bf16[256,3072]{1,0:T(8,128)(2,1)} %shard_map.150.refs_0_), channel_id=1, source_target_pairs={{0,2},{1,3},{2,0},{3,1},{4,6},{5,7},{6,4},{7,5}} | collective-permute-start | bytes 4718600 | tf_op jit(solution)/shard_map/ppermute | solution.py:343
  1249.0 69.8 %collective-permute-start.60 = (bf16[256,3072]{1,0:T(8,128)(2,1)}, bf16[256,3072]{1,0:T(8,128)(2,1)}, u32[]{:S(2)}, u32[]{:S(2)}) collective-permute-start(bf16[256,3072]{1,0:T(8,128)(2,1)} %shard_map.150.refs_0_), channel_id=1, source_target_pairs={{0,4},{1,5},{2,6},{3,7},{4,0},{5,1},{6,2},{7,3}} | collective-permute-start | bytes 4718600 | tf_op jit(solution)/shard_map/ppermute | solution.py:343
  1250.0 68.8 %collective-permute-start.101 = (bf16[256,3072]{1,0:T(8,128)(2,1)}, bf16[256,3072]{1,0:T(8,128)(2,1)S(1)}, u32[]{:S(2)}, u32[]{:S(2)}) collective-permute-start(bf16[256,3072]{1,0:T(8,128)(2,1)} %collective-permute-done.97.refs_1_), channel_id=1, source_target_pairs={{0,1},{1,0},{2,3},{3,2},{4,5},{5,4},{6,7},{7,6}} | collective-permute-start | bytes 4718600 | tf_op jit(solution)/shard_map/ppermute | solution.py:343
  1251.2 68.1 %collective-permute-start.102 = (bf16[256,3072]{1,0:T(8,128)(2,1)S(1)}, bf16[256,3072]{1,0:T(8,128)(2,1)S(1)}, u32[]{:S(2)}, u32[]{:S(2)}) collective-permute-start(bf16[256,3072]{1,0:T(8,128)(2,1)S(1)} %collective-permute-done.98.refs_2_), channel_id=1, source_target_pairs={{0,1},{1,0},{2,3},{3,2},{4,5},{5,4},{6,7},{7,6}} | collective-permute-start | bytes 4718600 | tf_op jit(solution)/shard_map/ppermute | solution.py:343
  1279.6 68.8 %collective-permute-start.61 = (bf16[256,3072]{1,0:T(8,128)(2,1)}, bf16[256,3072]{1,0:T(8,128)(2,1)}, u32[]{:S(2)}, u32[]{:S(2)}) collective-permute-start(bf16[256,3072]{1,0:T(8,128)(2,1)} %collective-permute-done.59.refs_1_), channel_id=1, source_target_pairs={{0,4},{1,5},{2,6},{3,7},{4,0},{5,1},{6,2},{7,3}} | collective-permute-start | bytes 4718600 | tf_op jit(solution)/shard_map/ppermute | solution.py:343
  1285.1 66.6 %collective-permute-start.103 = (bf16[256,3072]{1,0:T(8,128)(2,1)}, bf16[256,3072]{1,0:T(8,128)(2,1)}, u32[]{:S(2)}, u32[]{:S(2)}) collective-permute-start(bf16[256,3072]{1,0:T(8,128)(2,1)} %collective-permute-done.99.refs_3_), channel_id=1, source_target_pairs={{0,1},{1,0},{2,3},{3,2},{4,5},{5,4},{6,7},{7,6}} | collective-permute-start | bytes 4718600 | tf_op jit(solution)/shard_map/ppermute | solution.py:343
  1318.8 51.6 %collective-permute-start.62 = (bf16[256,3072]{1,0:T(8,128)(2,1)}, bf16[256,3072]{1,0:T(8,128)(2,1)}, u32[]{:S(2)}, u32[]{:S(2)}) collective-permute-start(bf16[256,3072]{1,0:T(8,128)(2,1)} %shard_map.150.refs_0_), channel_id=1, source_target_pairs={{0,1},{1,0},{2,3},{3,2},{4,5},{5,4},{6,7},{7,6}} | collective-permute-start | bytes 4718600 | tf_op jit(solution)/shard_map/ppermute | solution.py:343
  1318.8 51.7 %collective-permute-start.63 = (bf16[256,3072]{1,0:T(8,128)(2,1)}, bf16[256,3072]{1,0:T(8,128)(2,1)}, u32[]{:S(2)}, u32[]{:S(2)}) collective-permute-start(bf16[256,3072]{1,0:T(8,128)(2,1)} %collective-permute-done.59.refs_1_), channel_id=1, source_target_pairs={{0,1},{1,0},{2,3},{3,2},{4,5},{5,4},{6,7},{7,6}} | collective-permute-start | bytes 4718600 | tf_op jit(solution)/shard_map/ppermute | solution.py:343
  1319.3 51.6 %collective-permute-start.64 = (bf16[256,3072]{1,0:T(8,128)(2,1)}, bf16[256,3072]{1,0:T(8,128)(2,1)}, u32[]{:S(2)}, u32[]{:S(2)}) collective-permute-start(bf16[256,3072]{1,0:T(8,128)(2,1)} %collective-permute-done.60.refs_2_), channel_id=1, source_target_pairs={{0,1},{1,0},{2,3},{3,2},{4,5},{5,4},{6,7},{7,6}} | collective-permute-start | bytes 4718600 | tf_op jit(solution)/shard_map/ppermute | solution.py:343
  (78 other events, 2358.5 us)
where the time goes:
time: 1410 us; the launch traced here: 1400 us
  Pallas kernels  737 us (52%)
  waiting for transfers between devices  530 us (38%)
  starting transfers between devices  76.5 us (5%)
  local copies, waits for them, and re-layouts  29 us (2%)
  other arithmetic  21.5 us (2%)
    ppermute x104, waiting for transfers between devices, swap(): return lax.ppermute(a, 'tp', [(i, i ^ bit) for i in range(tp)])  530 us
    pallas_call x10, Pallas kernels, _mlp(): pl.pallas_call(functools.partial(_mlp_kernel, fb, db), grid=(rows // bm,)...  233 us
    pallas_call x5, Pallas kernels, _attn(): pl.pallas_call(functools.partial(_attn_kernel, hl, q0, bq, bk), grid=(nq,...  191 us
    pallas_call x5, Pallas kernels, _h(): pl.pallas_call(functools.partial(_h_kernel, n, sizes), grid_spec=pltpu.Pr...  139 us
    ppermute x104, starting transfers between devices, swap(): return lax.ppermute(a, 'tp', [(i, i ^ bit) for i in range(tp)])  76.5 us
    pallas_call x15, Pallas kernels, _sums(): pl.pallas_call(functools.partial(_sum_kernel, tuple((len(g) for g in term...  73.6 us
    pallas_call x1, Pallas kernels, _qkv(): pl.pallas_call(functools.partial(_qkv_kernel, hl), grid=(t // bm,), in_sp...  57.9 us
    pallas_call x5, Pallas kernels, _place(): pl.pallas_call(functools.partial(_place_kernel, n), grid_spec=pltpu.Prefe...  42.3 us
  transfers between devices with their start and end apart: 104, of which 24 were waited for; matrix products, arithmetic and copies ran while one was open for 1% of the time, Pallas kernels for 45%

commit v1 on v0

--- a/solution.py
+++ b/solution.py
@@ -12,7 +12,7 @@
 EPS = 1e-5
 ROPE_BASE = 500000.0
 LOG2E = 1.4426950408889634
-CHUNKS = (2048, 1536, 2048, 1536, 1024)
+CHUNKS = (2048, 2048, 2048, 1024, 1024)
 VMEM = 62 << 20
 F32, BF = jnp.float32, jnp.bfloat16
 
@@ -20,7 +20,9 @@
 def _cs(pos):
     half = HEAD // 2
     inv = ROPE_BASE ** (-2.0 * jnp.arange(half, dtype=F32) / HEAD)
-    ang = pos.astype(F32)[:, None] * inv
+    p = pos.astype(F32).reshape(2, -1, 1)
+    low = lax.broadcasted_iota(jnp.int32, (1, HEAD), 1) < half
+    ang = jnp.where(low, p[0], p[1]) * jnp.tile(inv, 2)
     return jnp.cos(ang), jnp.sin(ang)
 
 
@@ -29,9 +31,16 @@
     inv = lax.rsqrt(jnp.mean(x * x, axis=-1, keepdims=True) + EPS)
     a = (x * inv * g_ref[...].astype(F32)).astype(BF)
     r = jnp.dot(a, w_ref[...], preferred_element_type=F32)
-    c, s = c_ref[...], s_ref[...]
-    cc = jnp.concatenate([c, c], axis=-1)
-    ss = jnp.concatenate([-s, s], axis=-1)
+    low = lax.broadcasted_iota(jnp.int32, c_ref.shape, 1) < HEAD // 2
+    first = pl.program_id(0) < pl.num_programs(0) // 2
+    here = jnp.logical_xor(low, jnp.logical_not(first))
+
+    def both(ref):
+        t = ref[...]
+        return jnp.where(here, t, pltpu.roll(t, HEAD // 2, 1))
+
+    cc, ss = both(c_ref), both(s_ref)
+    ss = jnp.where(low, -ss, ss)
     for n in range(hl + 1):
         t = r[:, n * HEAD:(n + 1) * HEAD]
         t = (t * cc + pltpu.roll(t, HEAD // 2, 1) * ss).astype(BF)
@@ -44,7 +53,8 @@
 
 def _qkv(x, g1, w, c, s, hl):
     t, d = x.shape
-    bm = min(t, 512)
+    bm = min(t // 2, 512)
+    nb = t // 2 // bm
     n = w.shape[1]
     row = lambda i: (i, 0)
     fix = lambda i: (0, 0)
@@ -55,8 +65,8 @@
             pl.BlockSpec((bm, d), row),
             pl.BlockSpec((1, d), fix),
             pl.BlockSpec((d, n), fix),
-            pl.BlockSpec((bm, HEAD // 2), row),
-            pl.BlockSpec((bm, HEAD // 2), row),
+            pl.BlockSpec((bm, HEAD), lambda i: (i % nb, 0)),
+            pl.BlockSpec((bm, HEAD), lambda i: (i % nb, 0)),
         ],
         out_specs=[
             pl.BlockSpec((bm, hl * HEAD), row),
@@ -141,7 +151,7 @@
         out_specs=pl.BlockSpec((bq, hl * HEAD), lambda i: (i, 0)),
         out_shape=jax.ShapeDtypeStruct((rows, hl * HEAD), BF),
         scratch_shapes=[pltpu.VMEM((hl, bq, HEAD), F32)] * 3,
-        compiler_params=pltpu.CompilerParams(vmem_limit_bytes=VMEM),
+        compiler_params=pltpu.CompilerParams(vmem_limit_bytes=40 << 20),
         cost_estimate=pl.CostEstimate(
             flops=4 * 3 * HEAD * hl * area, bytes_accessed=4 * end * HEAD, transcendentals=hl * area),
     )(q, kt, v)

time: 1410 us -> 1270 us (0.901)
  waiting for transfers between devices: 530 us -> 430 us
  Pallas kernels: 737 us -> 719 us
    ppermute x104, waiting for transfers between devices: 530 us -> 430 us  [swap(): return lax.ppermute(a, 'tp', [(i, i ^ bit) for i in range(tp)])]
    pallas_call x5, Pallas kernels: 191 us -> 175 us  [_attn(): pl.pallas_call(functools.partial(_attn_kernel, hl, q0, bq, bk), grid=(nq,...]
  transfers between devices with their start and end apart: 104 -> 104, of which waited for: 24 -> 22; matrix products, arithmetic and copies ran while one was open for 1% -> 1% of each run, Pallas kernels for 45% -> 49%
where the time goes in v1:
time: 1270 us; the launch traced here: 1260 us
  Pallas kernels  719 us (57%)
  waiting for transfers between devices  430 us (34%)
  starting transfers between devices  73.1 us (6%)
  local copies, waits for them, and re-layouts  26.4 us (2%)
  other arithmetic  13.2 us (1%)
    ppermute x104, waiting for transfers between devices, swap(): return lax.ppermute(a, 'tp', [(i, i ^ bit) for i in range(tp)])  430 us
    pallas_call x10, Pallas kernels, _mlp(): pl.pallas_call(functools.partial(_mlp_kernel, fb, db), grid=(rows // bm,)...  233 us
    pallas_call x5, Pallas kernels, _attn(): pl.pallas_call(functools.partial(_attn_kernel, hl, q0, bq, bk), grid=(nq,...  175 us
    pallas_call x5, Pallas kernels, _h(): pl.pallas_call(functools.partial(_h_kernel, n, sizes), grid_spec=pltpu.Pr...  139 us
    ppermute x104, starting transfers between devices, swap(): return lax.ppermute(a, 'tp', [(i, i ^ bit) for i in range(tp)])  73.1 us
    pallas_call x15, Pallas kernels, _sums(): pl.pallas_call(functools.partial(_sum_kernel, tuple((len(g) for g in term...  70.8 us
    pallas_call x1, Pallas kernels, _qkv(): pl.pallas_call(functools.partial(_qkv_kernel, hl), grid=(t // bm,), in_sp...  58.1 us
    pallas_call x5, Pallas kernels, _place(): pl.pallas_call(functools.partial(_place_kernel, n), grid_spec=pltpu.Prefe...  42.4 us
  transfers between devices with their start and end apart: 104, of which 22 were waited for; matrix products, arithmetic and copies ran while one was open for 1% of the time, Pallas kernels for 49%

profile of v1, /device:TPU:0, one launch (start us, length us, event | category | flops | bytes accessed | tf_op | source)
XLA Modules:
  0.0 1263.9 jit_solution(1163624489219798869)
XLA Ops:
  6.7 9.4 fusion
  16.1 58.1 %qkv.1 = (bf16[8192,384]{1,0:T(8,128)(2,1)}, bf16[8192,128]{1,0:T(8,128)(2,1)}, bf16[8192,128]{1,0:T(8,128)(2,1)}) custom-call(bf16[8192,3072]{1,0:T(8,128)(2,1)} %x_ref.11, bf16[1,3072]{1,0:T(2,128)(2,1)} %reshape.57.g_ref, bf16[3072,640]{1,0:T(8,128)(2,1)} %pad_maximum_fusion.w_ref, f32[4096,128]{1,0:T(8,128)} %get-tuple-element.60.c_ref, ...), custom_call_target="tpu_custom_call" | custom-call | flops 32212254720 | bytes 50331648 | tf_op jit(solution)/shard_map/qkv/pallas_call | solution.py:61
  74.3 2.9 copy.18
  81.6 34.4 %shard_map.137 = bf16[1024,384]{1,0:T(8,128)(2,1)S(1)} custom-call(bf16[8192,384]{1,0:T(8,128)(2,1)S(1)} %copy-done.3, bf16[128,8192]{1,0:T(8,128)(2,1)S(1)} %bitcast.52, bf16[8192,128]{1,0:T(8,128)(2,1)S(1)} %copy-done.1), custom_call_target="tpu_custom_call" | custom-call | flops 32614907904 | bytes 3670016 | tf_op jit(solution)/shard_map/pallas_call | solution.py:143
  116.8 3.3 collective-permute-start.29
  121.6 39.4 %shard_map.130 = bf16[1024,384]{1,0:T(8,128)(2,1)S(1)} custom-call(bf16[8192,384]{1,0:T(8,128)(2,1)S(1)} %copy-done.3, bf16[128,8192]{1,0:T(8,128)(2,1)S(1)} %bitcast.53, bf16[8192,128]{1,0:T(8,128)(2,1)S(1)} %copy-done.1), custom_call_target="tpu_custom_call" | custom-call | flops 37446746112 | bytes 4194304 | tf_op jit(solution)/shard_map/pallas_call | solution.py:143
  162.4 13.9 %shard_map.158 = bf16[2048,384]{1,0:T(8,128)(2,1)S(1)} custom-call(bf16[8192,384]{1,0:T(8,128)(2,1)S(1)} %copy-done.3, bf16[128,8192]{1,0:T(8,128)(2,1)S(1)} %bitcast.54, bf16[8192,128]{1,0:T(8,128)(2,1)S(1)} %copy-done.1), custom_call_target="tpu_custom_call" | custom-call | flops 12079595520 | bytes 1048576 | tf_op jit(solution)/shard_map/pallas_call | solution.py:143
  184.6 33.8 %shard_map.151 = bf16[2048,384]{1,0:T(8,128)(2,1)S(1)} custom-call(bf16[8192,384]{1,0:T(8,128)(2,1)S(1)} %copy-done.4, bf16[128,8192]{1,0:T(8,128)(2,1)S(1)} %bitcast.55, bf16[8192,128]{1,0:T(8,128)(2,1)S(1)} %copy-done.2), custom_call_target="tpu_custom_call" | custom-call | flops 31406948352 | bytes 2097152 | tf_op jit(solution)/shard_map/pallas_call | solution.py:143
  222.7 53.8 %shard_map.144 = bf16[2048,384]{1,0:T(8,128)(2,1)S(1)} custom-call(bf16[8192,384]{1,0:T(8,128)(2,1)S(1)} %copy-done.4, bf16[128,8192]{1,0:T(8,128)(2,1)S(1)} %bitcast.56, bf16[8192,128]{1,0:T(8,128)(2,1)S(1)} %copy-done.2), custom_call_target="tpu_custom_call" | custom-call | flops 50734301184 | bytes 3145728 | tf_op jit(solution)/shard_map/pallas_call | solution.py:143
  278.2 12.3 collective-permute-done.67.refs_2_
  291.0 15.4 %collective-permute-done.69.refs_4_ = bf16[1024,384]{1,0:T(8,128)(2,1)S(1)} collective-permute-done((bf16[1024,384]{1,0:T(8,128)(2,1)S(1)}, bf16[1024,384]{1,0:T(8,128)(2,1)S(1)}, u32[]{:S(2)}, u32[]{:S(2)}) %collective-permute-start.69) | collective-permute-done | bytes 786464 | tf_op jit(solution)/shard_map/ppermute | solution.py:353
  308.5 14.8 %collective-permute-done.89.refs_5_ = bf16[1024,384]{1,0:T(8,128)(2,1)S(1)} collective-permute-done((bf16[1024,384]{1,0:T(8,128)(2,1)S(1)}, bf16[1024,384]{1,0:T(8,128)(2,1)S(1)}, u32[]{:S(2)}, u32[]{:S(2)}) %collective-permute-start.89) | collective-permute-done | bytes 786464 | tf_op jit(solution)/shard_map/ppermute | solution.py:353
  328.2 11.9 collective-permute-done.90.refs_6_
  340.2 16.8 %collective-permute-done.70.refs_5_ = bf16[1024,384]{1,0:T(8,128)(2,1)S(1)} collective-permute-done((bf16[1024,384]{1,0:T(8,128)(2,1)S(1)}, bf16[1024,384]{1,0:T(8,128)(2,1)S(1)}, u32[]{:S(2)}, u32[]{:S(2)}) %collective-permute-start.70) | collective-permute-done | bytes 786464 | tf_op jit(solution)/shard_map/ppermute | solution.py:353
  357.5 24.3 %collective-permute-done.12.refs_14_ = bf16[192,3072]{1,0:T(8,128)(2,1)S(1)} collective-permute-done((bf16[192,3072]{1,0:T(8,128)(2,1)S(1)}, bf16[192,3072]{1,0:T(8,128)(2,1)S(1)}, u32[]{:S(2)}, u32[]{:S(2)}) %collective-permute-start.12) | collective-permute-done | bytes 1179680 | tf_op jit(solution)/shard_map/ppermute | solution.py:353
  390.0 32.4 %shard_map.159 = (bf16[1024,3072]{1,0:T(8,128)(2,1)}, bf16[1024,3072]{1,0:T(8,128)(2,1)}) custom-call(s32[1]{0:T(128)} %bitcast.49.off_ref, bf16[8192,3072]{1,0:T(8,128)(2,1)} %x_ref.11, bf16[1,3072]{1,0:T(2,128)(2,1)} %reshape.56.g_ref, bf16[1024,384]{1,0:T(8,128)(2,1)} %copy-done.13, bf16[1024,384]{1,0:T(8,128)(2,1)} %copy-done.26, ...), custom_call_target="tpu_custom_call" | custom-call | flops 19327352832 | bytes 44040192 | tf_op jit(solution)/shard_map/pallas_call | solution.py:191
  425.3 12.1 collective-permute-done.72.refs_7_
  437.8 32.5 %shard_map.152 = (bf16[1024,3072]{1,0:T(8,128)(2,1)}, bf16[1024,3072]{1,0:T(8,128)(2,1)}) custom-call(s32[1]{0:T(128)} %bitcast.40.off_ref, bf16[8192,3072]{1,0:T(8,128)(2,1)} %x_ref.11, bf16[1,3072]{1,0:T(2,128)(2,1)} %reshape.56.g_ref, bf16[1024,384]{1,0:T(8,128)(2,1)} %copy-done.12, bf16[1024,384]{1,0:T(8,128)(2,1)} %copy-done.27, ...), custom_call_target="tpu_custom_call" | custom-call | flops 19327352832 | bytes 44040192 | tf_op jit(solution)/shard_map/pallas_call | solution.py:191
  474.3 21.4 %shard_map.138 = (bf16[512,3072]{1,0:T(8,128)(2,1)}, bf16[512,3072]{1,0:T(8,128)(2,1)}) custom-call(s32[1]{0:T(128)} %bitcast.22.off_ref, bf16[8192,3072]{1,0:T(8,128)(2,1)} %x_ref.11, bf16[1,3072]{1,0:T(2,128)(2,1)} %reshape.56.g_ref, bf16[512,384]{1,0:T(8,128)(2,1)} %copy-done.16, bf16[512,384]{1,0:T(8,128)(2,1)} %collective-permute-done.28.refs_1_, ...), custom_call_target="tpu_custom_call" | custom-call | flops 9663676416 | bytes 31457280 | tf_op jit(solution)/shard_map/pallas_call | solution.py:191
  499.6 20.9 %shard_map.131 = (bf16[512,3072]{1,0:T(8,128)(2,1)}, bf16[512,3072]{1,0:T(8,128)(2,1)}) custom-call(s32[1]{0:T(128)} %bitcast.12.off_ref, bf16[8192,3072]{1,0:T(8,128)(2,1)} %x_ref.11, bf16[1,3072]{1,0:T(2,128)(2,1)} %reshape.56.g_ref, bf16[512,384]{1,0:T(8,128)(2,1)} %copy-done.15, bf16[512,384]{1,0:T(8,128)(2,1)} %copy-done.43, ...), custom_call_target="tpu_custom_call" | custom-call | flops 9663676416 | bytes 31457280 | tf_op jit(solution)/shard_map/pallas_call | solution.py:191
  521.1 11.6 collective-permute-done.53.refs_7_
  532.7 32.3 %shard_map.145 = (bf16[1024,3072]{1,0:T(8,128)(2,1)}, bf16[1024,3072]{1,0:T(8,128)(2,1)}) custom-call(s32[1]{0:T(128)} %bitcast.31.off_ref, bf16[8192,3072]{1,0:T(8,128)(2,1)} %x_ref.11, bf16[1,3072]{1,0:T(2,128)(2,1)} %reshape.56.g_ref, bf16[1024,384]{1,0:T(8,128)(2,1)} %copy-done.11, bf16[1024,384]{1,0:T(8,128)(2,1)} %copy-done.22, ...), custom_call_target="tpu_custom_call" | custom-call | flops 19327352832 | bytes 44040192 | tf_op jit(solution)/shard_map/pallas_call | solution.py:191
  565.0 16.7 %shard_map.140 = bf16[512,3072]{1,0:T(8,128)(2,1)} custom-call(bf16[512,3072]{1,0:T(8,128)(2,1)} %collective-permute-done.35.b_ref, bf16[3072,1024]{1,0:T(8,128)(2,1)} %wg_ref.19, bf16[3072,1024]{1,0:T(8,128)(2,1)} %wu_ref.19, bf16[1024,3072]{1,0:T(8,128)(2,1)} %wd_ref.19), custom_call_target="tpu_custom_call" | custom-call | flops 9663676416 | bytes 25165824 | tf_op jit(solution)/shard_map/pallas_call | solution.py:260
  582.2 16.9 %shard_map.133 = bf16[512,3072]{1,0:T(8,128)(2,1)} custom-call(bf16[512,3072]{1,0:T(8,128)(2,1)} %collective-permute-done.16.b_ref, bf16[3072,1024]{1,0:T(8,128)(2,1)} %wg_ref.19, bf16[3072,1024]{1,0:T(8,128)(2,1)} %wu_ref.19, bf16[1024,3072]{1,0:T(8,128)(2,1)} %wd_ref.19), custom_call_target="tpu_custom_call" | custom-call | flops 9663676416 | bytes 25165824 | tf_op jit(solution)/shard_map/pallas_call | solution.py:260
  599.2 27.5 %shard_map.161 = bf16[1024,3072]{1,0:T(8,128)(2,1)} custom-call(bf16[1024,3072]{1,0:T(8,128)(2,1)} %collective-permute-done.92.b_ref, bf16[3072,1024]{1,0:T(8,128)(2,1)} %wg_ref.19, bf16[3072,1024]{1,0:T(8,128)(2,1)} %wu_ref.19, bf16[1024,3072]{1,0:T(8,128)(2,1)} %wd_ref.19), custom_call_target="tpu_custom_call" | custom-call | flops 19327352832 | bytes 31457280 | tf_op jit(solution)/shard_map/pallas_call | solution.py:260
  627.2 27.9 %shard_map.154 = bf16[1024,3072]{1,0:T(8,128)(2,1)} custom-call(bf16[1024,3072]{1,0:T(8,128)(2,1)} %collective-permute-done.73.b_ref, bf16[3072,1024]{1,0:T(8,128)(2,1)} %wg_ref.19, bf16[3072,1024]{1,0:T(8,128)(2,1)} %wu_ref.19, bf16[1024,3072]{1,0:T(8,128)(2,1)} %wd_ref.19), custom_call_target="tpu_custom_call" | custom-call | flops 19327352832 | bytes 31457280 | tf_op jit(solution)/shard_map/pallas_call | solution.py:260
  655.2 27.7 %shard_map.147 = bf16[1024,3072]{1,0:T(8,128)(2,1)} custom-call(bf16[1024,3072]{1,0:T(8,128)(2,1)} %collective-permute-done.54.b_ref, bf16[3072,1024]{1,0:T(8,128)(2,1)} %wg_ref.19, bf16[3072,1024]{1,0:T(8,128)(2,1)} %wu_ref.19, bf16[1024,3072]{1,0:T(8,128)(2,1)} %wd_ref.19), custom_call_target="tpu_custom_call" | custom-call | flops 19327352832 | bytes 31457280 | tf_op jit(solution)/shard_map/pallas_call | solution.py:260
  684.0 16.7 %shard_map.139.refs_0_.refs_2_ = bf16[512,3072]{1,0:T(8,128)(2,1)} custom-call(bf16[512,3072]{1,0:T(8,128)(2,1)} %get-tuple-element.33.b_ref, bf16[3072,1024]{1,0:T(8,128)(2,1)} %wg_ref.19, bf16[3072,1024]{1,0:T(8,128)(2,1)} %wu_ref.19, bf16[1024,3072]{1,0:T(8,128)(2,1)} %wd_ref.19), custom_call_target="tpu_custom_call" | custom-call | flops 9663676416 | bytes 25165824 | tf_op jit(solution)/shard_map/pallas_call | solution.py:260
  700.6 16.9 %shard_map.132.refs_0_.refs_2_ = bf16[512,3072]{1,0:T(8,128)(2,1)} custom-call(bf16[512,3072]{1,0:T(8,128)(2,1)} %get-tuple-element.29.b_ref, bf16[3072,1024]{1,0:T(8,128)(2,1)} %wg_ref.19, bf16[3072,1024]{1,0:T(8,128)(2,1)} %wu_ref.19, bf16[1024,3072]{1,0:T(8,128)(2,1)} %wd_ref.19), custom_call_target="tpu_custom_call" | custom-call | flops 9663676416 | bytes 25165824 | tf_op jit(solution)/shard_map/pallas_call | solution.py:260
  717.6 3.6 shard_map.141
  722.9 3.6 shard_map.134
  727.9 27.5 %shard_map.160.refs_0_.refs_2_ = bf16[1024,3072]{1,0:T(8,128)(2,1)} custom-call(bf16[1024,3072]{1,0:T(8,128)(2,1)} %get-tuple-element.45.b_ref, bf16[3072,1024]{1,0:T(8,128)(2,1)} %wg_ref.19, bf16[3072,1024]{1,0:T(8,128)(2,1)} %wu_ref.19, bf16[1024,3072]{1,0:T(8,128)(2,1)} %wd_ref.19), custom_call_target="tpu_custom_call" | custom-call | flops 19327352832 | bytes 31457280 | tf_op jit(solution)/shard_map/pallas_call | solution.py:260
  756.4 3.2 shard_map.142
  760.1 27.9 %shard_map.153.refs_0_.refs_2_ = bf16[1024,3072]{1,0:T(8,128)(2,1)} custom-call(bf16[1024,3072]{1,0:T(8,128)(2,1)} %get-tuple-element.41.b_ref, bf16[3072,1024]{1,0:T(8,128)(2,1)} %wg_ref.19, bf16[3072,1024]{1,0:T(8,128)(2,1)} %wu_ref.19, bf16[1024,3072]{1,0:T(8,128)(2,1)} %wd_ref.19), custom_call_target="tpu_custom_call" | custom-call | flops 19327352832 | bytes 31457280 | tf_op jit(solution)/shard_map/pallas_call | solution.py:260
  788.0 3.2 shard_map.135
  793.8 3.7 shard_map.143.refs_0_
  798.4 5.6 shard_map.162
  804.6 5.6 shard_map.155
  811.4 27.6 %shard_map.146.refs_0_.refs_2_ = bf16[1024,3072]{1,0:T(8,128)(2,1)} custom-call(bf16[1024,3072]{1,0:T(8,128)(2,1)} %get-tuple-element.37.b_ref, bf16[3072,1024]{1,0:T(8,128)(2,1)} %wg_ref.19, bf16[3072,1024]{1,0:T(8,128)(2,1)} %wu_ref.19, bf16[1024,3072]{1,0:T(8,128)(2,1)} %wd_ref.19), custom_call_target="tpu_custom_call" | custom-call | flops 19327352832 | bytes 31457280 | tf_op jit(solution)/shard_map/pallas_call | solution.py:260
  839.0 5.7 shard_map.148
  846.3 5.0 shard_map.163
  854.3 11.1 collective-permute-done.41.refs_2_
  865.3 3.8 shard_map.136.refs_0_
  870.6 5.0 shard_map.156
  876.5 70.0 %collective-permute-done.21.refs_1_ = bf16[128,3072]{1,0:T(8,128)(2,1)} collective-permute-done((bf16[128,3072]{1,0:T(8,128)(2,1)}, bf16[128,3072]{1,0:T(8,128)(2,1)}, u32[]{:S(2)}, u32[]{:S(2)}) %collective-permute-start.21) | collective-permute-done | bytes 786464 | tf_op jit(solution)/shard_map/ppermute | solution.py:353
  949.5 5.0 shard_map.149
  954.5 5.9 shard_map.164.refs_0_
  960.4 3.7 collective-permute-done.22.refs_2_
  964.6 36.4 %collective-permute-done.42.refs_3_ = bf16[128,3072]{1,0:T(8,128)(2,1)} collective-permute-done((bf16[128,3072]{1,0:T(8,128)(2,1)}, bf16[128,3072]{1,0:T(8,128)(2,1)}, u32[]{:S(2)}, u32[]{:S(2)}) %collective-permute-start.42) | collective-permute-done | bytes 786464 | tf_op jit(solution)/shard_map/ppermute | solution.py:353
  1004.5 6.0 shard_map.157.refs_0_
  1011.5 44.0 %collective-permute-done.23.refs_3_ = bf16[128,3072]{1,0:T(8,128)(2,1)} collective-permute-done((bf16[128,3072]{1,0:T(8,128)(2,1)}, bf16[128,3072]{1,0:T(8,128)(2,1)}, u32[]{:S(2)}, u32[]{:S(2)}) %collective-permute-start.23) | collective-permute-done | bytes 786464 | tf_op jit(solution)/shard_map/ppermute | solution.py:353
  1057.8 10.6 collective-permute-done.97.refs_1_
  1068.4 5.9 shard_map.150.refs_0_
  1074.3 14.9 %collective-permute-done.98.refs_2_ = bf16[256,3072]{1,0:T(8,128)(2,1)} collective-permute-done((bf16[256,3072]{1,0:T(8,128)(2,1)S(1)}, bf16[256,3072]{1,0:T(8,128)(2,1)}, u32[]{:S(2)}, u32[]{:S(2)}) %collective-permute-start.98) | collective-permute-done | bytes 1572896 | tf_op jit(solution)/shard_map/ppermute | solution.py:353
  1091.5 31.3 %collective-permute-done.78.refs_1_ = bf16[256,3072]{1,0:T(8,128)(2,1)} collective-permute-done((bf16[256,3072]{1,0:T(8,128)(2,1)}, bf16[256,3072]{1,0:T(8,128)(2,1)}, u32[]{:S(2)}, u32[]{:S(2)}) %collective-permute-start.78) | collective-permute-done | bytes 1572896 | tf_op jit(solution)/shard_map/ppermute | solution.py:353
  1124.0 7.9 collective-permute-done.59.refs_1_
  1131.8 24.7 %collective-permute-done.60.refs_2_ = bf16[256,3072]{1,0:T(8,128)(2,1)} collective-permute-done((bf16[256,3072]{1,0:T(8,128)(2,1)}, bf16[256,3072]{1,0:T(8,128)(2,1)}, u32[]{:S(2)}, u32[]{:S(2)}) %collective-permute-start.60) | collective-permute-done | bytes 1572896 | tf_op jit(solution)/shard_map/ppermute | solution.py:353
  1158.0 29.1 %collective-permute-done.99.refs_3_ = bf16[256,3072]{1,0:T(8,128)(2,1)S(1)} collective-permute-done((bf16[256,3072]{1,0:T(8,128)(2,1)}, bf16[256,3072]{1,0:T(8,128)(2,1)S(1)}, u32[]{:S(2)}, u32[]{:S(2)}) %collective-permute-start.99) | collective-permute-done | bytes 1572896 | tf_op jit(solution)/shard_map/ppermute | solution.py:353
  1189.3 25.8 %collective-permute-done.61.refs_3_ = bf16[256,3072]{1,0:T(8,128)(2,1)} collective-permute-done((bf16[256,3072]{1,0:T(8,128)(2,1)}, bf16[256,3072]{1,0:T(8,128)(2,1)}, u32[]{:S(2)}, u32[]{:S(2)}) %collective-permute-start.61) | collective-permute-done | bytes 1572896 | tf_op jit(solution)/shard_map/ppermute | solution.py:353
  1220.0 10.1 shard_map.165.refs_8_
  1231.3 10.0 shard_map.166.refs_8_
  1241.3 10.0 shard_map.167.refs_8_
  1251.3 6.2 shard_map.168.refs_8_
  1257.5 6.2 shard_map.169
  (302 shorter events, 98.8 us)
Async XLA Ops:
  116.8 62.9 %collective-permute-start.29 = (bf16[512,384]{1,0:T(8,128)(2,1)S(1)}, bf16[512,384]{1,0:T(8,128)(2,1)}, u32[]{:S(2)}, u32[]{:S(2)}) collective-permute-start(bf16[512,384]{1,0:T(8,128)(2,1)S(1)} %get-tuple-element.56.refs_0_), channel_id=1, source_target_pairs={{0,2},{1,3},{2,0},{3,1},{4,6},{5,7},{6,4},{7,5}} | collective-permute-start | bytes 1179656 | tf_op jit(solution)/shard_map/ppermute | solution.py:353
  120.1 61.6 %collective-permute-start.31 = (bf16[512,384]{1,0:T(8,128)(2,1)S(1)}, bf16[512,384]{1,0:T(8,128)(2,1)}, u32[]{:S(2)}, u32[]{:S(2)}) collective-permute-start(bf16[512,384]{1,0:T(8,128)(2,1)S(1)} %get-tuple-element.56.refs_0_), channel_id=1, source_target_pairs={{0,4},{1,5},{2,6},{3,7},{4,0},{5,1},{6,2},{7,3}} | collective-permute-start | bytes 1179656 | tf_op jit(solution)/shard_map/ppermute | solution.py:353
  161.9 58.2 %collective-permute-start.1 = (bf16[512,384]{1,0:T(8,128)(2,1)S(1)}, bf16[512,384]{1,0:T(8,128)(2,1)S(1)}, u32[]{:S(2)}, u32[]{:S(2)}) collective-permute-start(bf16[512,384]{1,0:T(8,128)(2,1)S(1)} %get-tuple-element.58.refs_0_), channel_id=1, source_target_pairs={{0,2},{1,3},{2,0},{3,1},{4,6},{5,7},{6,4},{7,5}} | collective-permute-start | bytes 1179656 | tf_op jit(solution)/shard_map/ppermute | solution.py:353
  162.4 58.2 %collective-permute-start.3 = (bf16[512,384]{1,0:T(8,128)(2,1)S(1)}, bf16[512,384]{1,0:T(8,128)(2,1)}, u32[]{:S(2)}, u32[]{:S(2)}) collective-permute-start(bf16[512,384]{1,0:T(8,128)(2,1)S(1)} %get-tuple-element.58.refs_0_), channel_id=1, source_target_pairs={{0,4},{1,5},{2,6},{3,7},{4,0},{5,1},{6,2},{7,3}} | collective-permute-start | bytes 1179656 | tf_op jit(solution)/shard_map/ppermute | solution.py:353
  179.2 41.5 %collective-permute-start.85 = (bf16[1024,384]{1,0:T(8,128)(2,1)S(1)}, bf16[1024,384]{1,0:T(8,128)(2,1)S(1)}, u32[]{:S(2)}, u32[]{:S(2)}) collective-permute-start(bf16[1024,384]{1,0:T(8,128)(2,1)S(1)} %get-tuple-element.49), channel_id=1, source_target_pairs={{0,1},{1,0},{2,3},{3,2},{4,5},{5,4},{6,7},{7,6}} | collective-permute-start | bytes 2359304 | tf_op jit(solution)/shard_map/ppermute | solution.py:353
  179.7 40.9 %collective-permute-start.86 = (bf16[1024,384]{1,0:T(8,128)(2,1)S(1)}, bf16[1024,384]{1,0:T(8,128)(2,1)S(1)}, u32[]{:S(2)}, u32[]{:S(2)}) collective-permute-start(bf16[1024,384]{1,0:T(8,128)(2,1)S(1)} %get-tuple-element.50.refs_0_), channel_id=1, source_target_pairs={{0,2},{1,3},{2,0},{3,1},{4,6},{5,7},{6,4},{7,5}} | collective-permute-start | bytes 2359304 | tf_op jit(solution)/shard_map/ppermute | solution.py:353
  181.8 36.8 %collective-permute-start = (bf16[512,384]{1,0:T(8,128)(2,1)S(1)}, bf16[512,384]{1,0:T(8,128)(2,1)S(1)}, u32[]{:S(2)}, u32[]{:S(2)}) collective-permute-start(bf16[512,384]{1,0:T(8,128)(2,1)S(1)} %copy-done.44), channel_id=1, source_target_pairs={{0,1},{1,0},{2,3},{3,2},{4,5},{5,4},{6,7},{7,6}} | collective-permute-start | bytes 1179656 | tf_op jit(solution)/shard_map/ppermute | solution.py:353
  218.5 58.1 %collective-permute-start.88 = (bf16[1024,384]{1,0:T(8,128)(2,1)S(1)}, bf16[1024,384]{1,0:T(8,128)(2,1)S(1)}, u32[]{:S(2)}, u32[]{:S(2)}) collective-permute-start(bf16[1024,384]{1,0:T(8,128)(2,1)S(1)} %get-tuple-element.50.refs_0_), channel_id=1, source_target_pairs={{0,4},{1,5},{2,6},{3,7},{4,0},{5,1},{6,2},{7,3}} | collective-permute-start | bytes 2359304 | tf_op jit(solution)/shard_map/ppermute | solution.py:353
  220.1 104.7 %collective-permute-start.8 = (bf16[384,3072]{1,0:T(8,128)(2,1)}, bf16[384,3072]{1,0:T(8,128)(2,1)}, u32[]{:S(2)}, u32[]{:S(2)}) collective-permute-start(bf16[384,3072]{1,0:T(8,128)(2,1)} %refs_8_.9), channel_id=1, source_target_pairs={{0,2},{1,3},{2,0},{3,1},{4,6},{5,7},{6,4},{7,5}} | collective-permute-start | bytes 7077896 | tf_op jit(solution)/shard_map/ppermute | solution.py:353
  220.6 106.0 %collective-permute-start.10 = (bf16[384,3072]{1,0:T(8,128)(2,1)}, bf16[384,3072]{1,0:T(8,128)(2,1)}, u32[]{:S(2)}, u32[]{:S(2)}) collective-permute-start(bf16[384,3072]{1,0:T(8,128)(2,1)} %refs_8_.9), channel_id=1, source_target_pairs={{0,4},{1,5},{2,6},{3,7},{4,0},{5,1},{6,2},{7,3}} | collective-permute-start | bytes 7077896 | tf_op jit(solution)/shard_map/ppermute | solution.py:353
  220.7 57.5 %collective-permute-start.66 = (bf16[1024,384]{1,0:T(8,128)(2,1)S(1)}, bf16[1024,384]{1,0:T(8,128)(2,1)S(1)}, u32[]{:S(2)}, u32[]{:S(2)}) collective-permute-start(bf16[1024,384]{1,0:T(8,128)(2,1)S(1)} %get-tuple-element.51), channel_id=1, source_target_pairs={{0,1},{1,0},{2,3},{3,2},{4,5},{5,4},{6,7},{7,6}} | collective-permute-start | bytes 2359304 | tf_op jit(solution)/shard_map/ppermute | solution.py:353
  220.7 69.8 %collective-permute-start.67 = (bf16[1024,384]{1,0:T(8,128)(2,1)S(1)}, bf16[1024,384]{1,0:T(8,128)(2,1)S(1)}, u32[]{:S(2)}, u32[]{:S(2)}) collective-permute-start(bf16[1024,384]{1,0:T(8,128)(2,1)S(1)} %get-tuple-element.52.refs_0_), channel_id=1, source_target_pairs={{0,2},{1,3},{2,0},{3,1},{4,6},{5,7},{6,4},{7,5}} | collective-permute-start | bytes 2359304 | tf_op jit(solution)/shard_map/ppermute | solution.py:353
  326.7 56.6 %collective-permute-start.7 = (bf16[384,3072]{1,0:T(8,128)(2,1)}, bf16[384,3072]{1,0:T(8,128)(2,1)}, u32[]{:S(2)}, u32[]{:S(2)}) collective-permute-start(bf16[384,3072]{1,0:T(8,128)(2,1)} %refs_8_.9), channel_id=1, source_target_pairs={{0,1},{1,0},{2,3},{3,2},{4,5},{5,4},{6,7},{7,6}} | collective-permute-start | bytes 7077896 | tf_op jit(solution)/shard_map/ppermute | solution.py:353
  328.1 53.6 %collective-permute-start.12 = (bf16[192,3072]{1,0:T(8,128)(2,1)S(1)}, bf16[192,3072]{1,0:T(8,128)(2,1)S(1)}, u32[]{:S(2)}, u32[]{:S(2)}) collective-permute-start(bf16[192,3072]{1,0:T(8,128)(2,1)S(1)} %slice.20), channel_id=1, source_target_pairs={{0,4},{1,5},{2,6},{3,7},{4,0},{5,1},{6,2},{7,3}} | collective-permute-start | bytes 3538952 | tf_op jit(solution)/shard_map/ppermute | solution.py:353
  340.1 41.7 %collective-permute-start.13 = (bf16[192,3072]{1,0:T(8,128)(2,1)S(1)}, bf16[192,3072]{1,0:T(8,128)(2,1)S(1)}, u32[]{:S(2)}, u32[]{:S(2)}) collective-permute-start(bf16[192,3072]{1,0:T(8,128)(2,1)S(1)} %slice.21), channel_id=1, source_target_pairs={{0,2},{1,3},{2,0},{3,1},{4,6},{5,7},{6,4},{7,5}} | collective-permute-start | bytes 3538952 | tf_op jit(solution)/shard_map/ppermute | solution.py:353
  383.2 39.1 %collective-permute-start.48 = (bf16[1024,384]{1,0:T(8,128)(2,1)S(1)}, bf16[1024,384]{1,0:T(8,128)(2,1)}, u32[]{:S(2)}, u32[]{:S(2)}) collective-permute-start(bf16[1024,384]{1,0:T(8,128)(2,1)S(1)} %get-tuple-element.54.refs_0_), channel_id=1, source_target_pairs={{0,2},{1,3},{2,0},{3,1},{4,6},{5,7},{6,4},{7,5}} | collective-permute-start | bytes 2359304 | tf_op jit(solution)/shard_map/ppermute | solution.py:353
  384.7 38.2 %collective-permute-start.32 = (bf16[512,384]{1,0:T(8,128)(2,1)}, bf16[512,384]{1,0:T(8,128)(2,1)}, u32[]{:S(2)}, u32[]{:S(2)}) collective-permute-start(bf16[512,384]{1,0:T(8,128)(2,1)} %collective-permute-done.28.refs_1_), channel_id=1, source_target_pairs={{0,4},{1,5},{2,6},{3,7},{4,0},{5,1},{6,2},{7,3}} | collective-permute-start | bytes 1179656 | tf_op jit(solution)/shard_map/ppermute | solution.py:353
  386.4 36.9 %collective-permute-start.68 = (bf16[1024,384]{1,0:T(8,128)(2,1)}, bf16[1024,384]{1,0:T(8,128)(2,1)}, u32[]{:S(2)}, u32[]{:S(2)}) collective-permute-start(bf16[1024,384]{1,0:T(8,128)(2,1)} %copy-done.27), channel_id=1, source_target_pairs={{0,2},{1,3},{2,0},{3,1},{4,6},{5,7},{6,4},{7,5}} | collective-permute-start | bytes 2359304 | tf_op jit(solution)/shard_map/ppermute | solution.py:353
  386.8 38.2 %collective-permute-start.71 = (bf16[1024,384]{1,0:T(8,128)(2,1)}, bf16[1024,384]{1,0:T(8,128)(2,1)}, u32[]{:S(2)}, u32[]{:S(2)}) collective-permute-start(bf16[1024,384]{1,0:T(8,128)(2,1)} %copy-done.29), channel_id=1, source_target_pairs={{0,4},{1,5},{2,6},{3,7},{4,0},{5,1},{6,2},{7,3}} | collective-permute-start | bytes 2359304 | tf_op jit(solution)/shard_map/ppermute | solution.py:353
  388.5 49.0 %collective-permute-start.72 = (bf16[1024,384]{1,0:T(8,128)(2,1)}, bf16[1024,384]{1,0:T(8,128)(2,1)}, u32[]{:S(2)}, u32[]{:S(2)}) collective-permute-start(bf16[1024,384]{1,0:T(8,128)(2,1)} %copy-done.32), channel_id=1, source_target_pairs={{0,2},{1,3},{2,0},{3,1},{4,6},{5,7},{6,4},{7,5}} | collective-permute-start | bytes 2359304 | tf_op jit(solution)/shard_map/ppermute | solution.py:353
  422.4 47.8 %collective-permute-start.50 = (bf16[1024,384]{1,0:T(8,128)(2,1)S(1)}, bf16[1024,384]{1,0:T(8,128)(2,1)}, u32[]{:S(2)}, u32[]{:S(2)}) collective-permute-start(bf16[1024,384]{1,0:T(8,128)(2,1)S(1)} %get-tuple-element.54.refs_0_), channel_id=1, source_target_pairs={{0,4},{1,5},{2,6},{3,7},{4,0},{5,1},{6,2},{7,3}} | collective-permute-start | bytes 2359304 | tf_op jit(solution)/shard_map/ppermute | solution.py:353
  422.9 49.0 %collective-permute-start.30 = (bf16[512,384]{1,0:T(8,128)(2,1)}, bf16[512,384]{1,0:T(8,128)(2,1)}, u32[]{:S(2)}, u32[]{:S(2)}) collective-permute-start(bf16[512,384]{1,0:T(8,128)(2,1)} %collective-permute-done.28.refs_1_), channel_id=1, source_target_pairs={{0,2},{1,3},{2,0},{3,1},{4,6},{5,7},{6,4},{7,5}} | collective-permute-start | bytes 1179656 | tf_op jit(solution)/shard_map/ppermute | solution.py:353
  423.3 50.2 %collective-permute-start.33 = (bf16[512,384]{1,0:T(8,128)(2,1)}, bf16[512,384]{1,0:T(8,128)(2,1)}, u32[]{:S(2)}, u32[]{:S(2)}) collective-permute-start(bf16[512,384]{1,0:T(8,128)(2,1)} %collective-permute-done.29.refs_2_), channel_id=1, source_target_pairs={{0,4},{1,5},{2,6},{3,7},{4,0},{5,1},{6,2},{7,3}} | collective-permute-start | bytes 1179656 | tf_op jit(solution)/shard_map/ppermute | solution.py:353
  425.0 49.0 %collective-permute-start.4 = (bf16[512,384]{1,0:T(8,128)(2,1)}, bf16[512,384]{1,0:T(8,128)(2,1)}, u32[]{:S(2)}, u32[]{:S(2)}) collective-permute-start(bf16[512,384]{1,0:T(8,128)(2,1)} %copy-done.43), channel_id=1, source_target_pairs={{0,4},{1,5},{2,6},{3,7},{4,0},{5,1},{6,2},{7,3}} | collective-permute-start | bytes 1179656 | tf_op jit(solution)/shard_map/ppermute | solution.py:353
  437.4 36.9 %collective-permute-start.34 = (bf16[512,384]{1,0:T(8,128)(2,1)}, bf16[512,384]{1,0:T(8,128)(2,1)}, u32[]{:S(2)}, u32[]{:S(2)}) collective-permute-start(bf16[512,384]{1,0:T(8,128)(2,1)} %collective-permute-done.32.refs_5_), channel_id=1, source_target_pairs={{0,2},{1,3},{2,0},{3,1},{4,6},{5,7},{6,4},{7,5}} | collective-permute-start | bytes 1179656 | tf_op jit(solution)/shard_map/ppermute | solution.py:353
  474.3 124.8 %collective-permute-start.92 = (bf16[1024,3072]{1,0:T(8,128)(2,1)}, bf16[1024,3072]{1,0:T(8,128)(2,1)}, u32[]{:S(2)}, u32[]{:S(2)}) collective-permute-start(bf16[1024,3072]{1,0:T(8,128)(2,1)} %get-tuple-element.45.b_ref), channel_id=1, source_target_pairs={{0,1},{1,0},{2,3},{3,2},{4,5},{5,4},{6,7},{7,6}} | collective-permute-start | bytes 18874376 | tf_op jit(solution)/shard_map/ppermute | solution.py:353
  499.6 65.4 %collective-permute-start.35 = (bf16[512,3072]{1,0:T(8,128)(2,1)}, bf16[512,3072]{1,0:T(8,128)(2,1)}, u32[]{:S(2)}, u32[]{:S(2)}) collective-permute-start(bf16[512,3072]{1,0:T(8,128)(2,1)} %get-tuple-element.33.b_ref), channel_id=1, source_target_pairs={{0,1},{1,0},{2,3},{3,2},{4,5},{5,4},{6,7},{7,6}} | collective-permute-start | bytes 9437192 | tf_op jit(solution)/shard_map/ppermute | solution.py:353
  520.5 106.7 %collective-permute-start.73 = (bf16[1024,3072]{1,0:T(8,128)(2,1)}, bf16[1024,3072]{1,0:T(8,128)(2,1)}, u32[]{:S(2)}, u32[]{:S(2)}) collective-permute-start(bf16[1024,3072]{1,0:T(8,128)(2,1)} %get-tuple-element.41.b_ref), channel_id=1, source_target_pairs={{0,1},{1,0},{2,3},{3,2},{4,5},{5,4},{6,7},{7,6}} | collective-permute-start | bytes 18874376 | tf_op jit(solution)/shard_map/ppermute | solution.py:353
  521.1 61.1 %collective-permute-start.16 = (bf16[512,3072]{1,0:T(8,128)(2,1)}, bf16[512,3072]{1,0:T(8,128)(2,1)}, u32[]{:S(2)}, u32[]{:S(2)}) collective-permute-start(bf16[512,3072]{1,0:T(8,128)(2,1)} %get-tuple-element.29.b_ref), channel_id=1, source_target_pairs={{0,1},{1,0},{2,3},{3,2},{4,5},{5,4},{6,7},{7,6}} | collective-permute-start | bytes 9437192 | tf_op jit(solution)/shard_map/ppermute | solution.py:353
  565.0 90.2 %collective-permute-start.54 = (bf16[1024,3072]{1,0:T(8,128)(2,1)}, bf16[1024,3072]{1,0:T(8,128)(2,1)}, u32[]{:S(2)}, u32[]{:S(2)}) collective-permute-start(bf16[1024,3072]{1,0:T(8,128)(2,1)} %get-tuple-element.37.b_ref), channel_id=1, source_target_pairs={{0,1},{1,0},{2,3},{3,2},{4,5},{5,4},{6,7},{7,6}} | collective-permute-start | bytes 18874376 | tf_op jit(solution)/shard_map/ppermute | solution.py:353
  581.7 135.9 %collective-permute-start.36 = (bf16[512,3072]{1,0:T(8,128)(2,1)}, bf16[512,3072]{1,0:T(8,128)(2,1)}, u32[]{:S(2)}, u32[]{:S(2)}) collective-permute-start(bf16[512,3072]{1,0:T(8,128)(2,1)} %shard_map.140), channel_id=1, source_target_pairs={{0,1},{1,0},{2,3},{3,2},{4,5},{5,4},{6,7},{7,6}} | collective-permute-start | bytes 9437192 | tf_op jit(solution)/shard_map/ppermute | solution.py:353
  599.1 123.7 %collective-permute-start.17 = (bf16[512,3072]{1,0:T(8,128)(2,1)}, bf16[512,3072]{1,0:T(8,128)(2,1)}, u32[]{:S(2)}, u32[]{:S(2)}) collective-permute-start(bf16[512,3072]{1,0:T(8,128)(2,1)} %shard_map.133), channel_id=1, source_target_pairs={{0,1},{1,0},{2,3},{3,2},{4,5},{5,4},{6,7},{7,6}} | collective-permute-start | bytes 9437192 | tf_op jit(solution)/shard_map/ppermute | solution.py:353
  626.7 170.8 %collective-permute-start.93 = (bf16[1024,3072]{1,0:T(8,128)(2,1)}, bf16[1024,3072]{1,0:T(8,128)(2,1)}, u32[]{:S(2)}, u32[]{:S(2)}) collective-permute-start(bf16[1024,3072]{1,0:T(8,128)(2,1)} %shard_map.161), channel_id=1, source_target_pairs={{0,1},{1,0},{2,3},{3,2},{4,5},{5,4},{6,7},{7,6}} | collective-permute-start | bytes 18874376 | tf_op jit(solution)/shard_map/ppermute | solution.py:353
  655.1 149.0 %collective-permute-start.74 = (bf16[1024,3072]{1,0:T(8,128)(2,1)}, bf16[1024,3072]{1,0:T(8,128)(2,1)}, u32[]{:S(2)}, u32[]{:S(2)}) collective-permute-start(bf16[1024,3072]{1,0:T(8,128)(2,1)} %shard_map.154), channel_id=1, source_target_pairs={{0,1},{1,0},{2,3},{3,2},{4,5},{5,4},{6,7},{7,6}} | collective-permute-start | bytes 18874376 | tf_op jit(solution)/shard_map/ppermute | solution.py:353
  682.8 127.4 %collective-permute-start.55 = (bf16[1024,3072]{1,0:T(8,128)(2,1)}, bf16[1024,3072]{1,0:T(8,128)(2,1)}, u32[]{:S(2)}, u32[]{:S(2)}) collective-permute-start(bf16[1024,3072]{1,0:T(8,128)(2,1)} %shard_map.147), channel_id=1, source_target_pairs={{0,1},{1,0},{2,3},{3,2},{4,5},{5,4},{6,7},{7,6}} | collective-permute-start | bytes 18874376 | tf_op jit(solution)/shard_map/ppermute | solution.py:353
  791.1 60.2 %collective-permute-start.18 = (bf16[128,3072]{1,0:T(8,128)(2,1)}, bf16[128,3072]{1,0:T(8,128)(2,1)}, u32[]{:S(2)}, u32[]{:S(2)}) collective-permute-start(bf16[128,3072]{1,0:T(8,128)(2,1)} %get-tuple-element.30), channel_id=1, source_target_pairs={{0,2},{1,3},{2,0},{3,1},{4,6},{5,7},{6,4},{7,5}} | collective-permute-start | bytes 2359304 | tf_op jit(solution)/shard_map/ppermute | solution.py:353
  792.6 59.2 %collective-permute-start.20 = (bf16[128,3072]{1,0:T(8,128)(2,1)}, bf16[128,3072]{1,0:T(8,128)(2,1)}, u32[]{:S(2)}, u32[]{:S(2)}) collective-permute-start(bf16[128,3072]{1,0:T(8,128)(2,1)} %shard_map.135), channel_id=1, source_target_pairs={{0,4},{1,5},{2,6},{3,7},{4,0},{5,1},{6,2},{7,3}} | collective-permute-start | bytes 2359304 | tf_op jit(solution)/shard_map/ppermute | solution.py:353
  797.5 55.8 %collective-permute-start.40 = (bf16[128,3072]{1,0:T(8,128)(2,1)}, bf16[128,3072]{1,0:T(8,128)(2,1)S(1)}, u32[]{:S(2)}, u32[]{:S(2)}) collective-permute-start(bf16[128,3072]{1,0:T(8,128)(2,1)} %shard_map.143.refs_0_), channel_id=1, source_target_pairs={{0,4},{1,5},{2,6},{3,7},{4,0},{5,1},{6,2},{7,3}} | collective-permute-start | bytes 2359304 | tf_op jit(solution)/shard_map/ppermute | solution.py:353
  804.0 40.7 %collective-permute-start.95 = (bf16[256,3072]{1,0:T(8,128)(2,1)}, bf16[256,3072]{1,0:T(8,128)(2,1)}, u32[]{:S(2)}, u32[]{:S(2)}) collective-permute-start(bf16[256,3072]{1,0:T(8,128)(2,1)} %get-tuple-element.47), channel_id=1, source_target_pairs={{0,2},{1,3},{2,0},{3,1},{4,6},{5,7},{6,4},{7,5}} | collective-permute-start | bytes 4718600 | tf_op jit(solution)/shard_map/ppermute | solution.py:353
  810.2 58.8 %collective-permute-start.76 = (bf16[256,3072]{1,0:T(8,128)(2,1)}, bf16[256,3072]{1,0:T(8,128)(2,1)}, u32[]{:S(2)}, u32[]{:S(2)}) collective-permute-start(bf16[256,3072]{1,0:T(8,128)(2,1)} %get-tuple-element.43), channel_id=1, source_target_pairs={{0,4},{1,5},{2,6},{3,7},{4,0},{5,1},{6,2},{7,3}} | collective-permute-start | bytes 4718600 | tf_op jit(solution)/shard_map/ppermute | solution.py:353
  851.3 96.7 %collective-permute-start.94 = (bf16[256,3072]{1,0:T(8,128)(2,1)}, bf16[256,3072]{1,0:T(8,128)(2,1)}, u32[]{:S(2)}, u32[]{:S(2)}) collective-permute-start(bf16[256,3072]{1,0:T(8,128)(2,1)} %get-tuple-element.46), channel_id=1, source_target_pairs={{0,2},{1,3},{2,0},{3,1},{4,6},{5,7},{6,4},{7,5}} | collective-permute-start | bytes 4718600 | tf_op jit(solution)/shard_map/ppermute | solution.py:353
  851.9 97.1 %collective-permute-start.57 = (bf16[256,3072]{1,0:T(8,128)(2,1)}, bf16[256,3072]{1,0:T(8,128)(2,1)}, u32[]{:S(2)}, u32[]{:S(2)}) collective-permute-start(bf16[256,3072]{1,0:T(8,128)(2,1)} %get-tuple-element.39), channel_id=1, source_target_pairs={{0,2},{1,3},{2,0},{3,1},{4,6},{5,7},{6,4},{7,5}} | collective-permute-start | bytes 4718600 | tf_op jit(solution)/shard_map/ppermute | solution.py:353
  853.4 96.1 %collective-permute-start.96 = (bf16[256,3072]{1,0:T(8,128)(2,1)}, bf16[256,3072]{1,0:T(8,128)(2,1)}, u32[]{:S(2)}, u32[]{:S(2)}) collective-permute-start(bf16[256,3072]{1,0:T(8,128)(2,1)} %shard_map.163), channel_id=1, source_target_pairs={{0,4},{1,5},{2,6},{3,7},{4,0},{5,1},{6,2},{7,3}} | collective-permute-start | bytes 4718600 | tf_op jit(solution)/shard_map/ppermute | solution.py:353
  869.1 77.5 %collective-permute-start.21 = (bf16[128,3072]{1,0:T(8,128)(2,1)}, bf16[128,3072]{1,0:T(8,128)(2,1)}, u32[]{:S(2)}, u32[]{:S(2)}) collective-permute-start(bf16[128,3072]{1,0:T(8,128)(2,1)} %shard_map.136.refs_0_), channel_id=1, source_target_pairs={{0,2},{1,3},{2,0},{3,1},{4,6},{5,7},{6,4},{7,5}} | collective-permute-start | bytes 2359304 | tf_op jit(solution)/shard_map/ppermute | solution.py:353
  875.6 127.7 %collective-permute-start.75 = (bf16[256,3072]{1,0:T(8,128)(2,1)}, bf16[256,3072]{1,0:T(8,128)(2,1)}, u32[]{:S(2)}, u32[]{:S(2)}) collective-permute-start(bf16[256,3072]{1,0:T(8,128)(2,1)} %get-tuple-element.42), channel_id=1, source_target_pairs={{0,4},{1,5},{2,6},{3,7},{4,0},{5,1},{6,2},{7,3}} | collective-permute-start | bytes 4718600 | tf_op jit(solution)/shard_map/ppermute | solution.py:353
  946.6 56.8 %collective-permute-start.77 = (bf16[256,3072]{1,0:T(8,128)(2,1)}, bf16[256,3072]{1,0:T(8,128)(2,1)}, u32[]{:S(2)}, u32[]{:S(2)}) collective-permute-start(bf16[256,3072]{1,0:T(8,128)(2,1)} %shard_map.156), channel_id=1, source_target_pairs={{0,2},{1,3},{2,0},{3,1},{4,6},{5,7},{6,4},{7,5}} | collective-permute-start | bytes 4718600 | tf_op jit(solution)/shard_map/ppermute | solution.py:353
  948.9 52.0 %collective-permute-start.42 = (bf16[128,3072]{1,0:T(8,128)(2,1)}, bf16[128,3072]{1,0:T(8,128)(2,1)}, u32[]{:S(2)}, u32[]{:S(2)}) collective-permute-start(bf16[128,3072]{1,0:T(8,128)(2,1)} %copy-done.21), channel_id=1, source_target_pairs={{0,2},{1,3},{2,0},{3,1},{4,6},{5,7},{6,4},{7,5}} | collective-permute-start | bytes 2359304 | tf_op jit(solution)/shard_map/ppermute | solution.py:353
  949.5 52.4 %collective-permute-start.44 = (bf16[128,3072]{1,0:T(8,128)(2,1)}, bf16[128,3072]{1,0:T(8,128)(2,1)}, u32[]{:S(2)}, u32[]{:S(2)}) collective-permute-start(bf16[128,3072]{1,0:T(8,128)(2,1)} %copy-done.21), channel_id=1, source_target_pairs={{0,1},{1,0},{2,3},{3,2},{4,5},{5,4},{6,7},{7,6}} | collective-permute-start | bytes 2359304 | tf_op jit(solution)/shard_map/ppermute | solution.py:353
  964.1 91.3 %collective-permute-start.56 = (bf16[256,3072]{1,0:T(8,128)(2,1)}, bf16[256,3072]{1,0:T(8,128)(2,1)}, u32[]{:S(2)}, u32[]{:S(2)}) collective-permute-start(bf16[256,3072]{1,0:T(8,128)(2,1)} %get-tuple-element.38), channel_id=1, source_target_pairs={{0,2},{1,3},{2,0},{3,1},{4,6},{5,7},{6,4},{7,5}} | collective-permute-start | bytes 4718600 | tf_op jit(solution)/shard_map/ppermute | solution.py:353
  1001.0 55.3 %collective-permute-start.58 = (bf16[256,3072]{1,0:T(8,128)(2,1)}, bf16[256,3072]{1,0:T(8,128)(2,1)}, u32[]{:S(2)}, u32[]{:S(2)}) collective-permute-start(bf16[256,3072]{1,0:T(8,128)(2,1)} %shard_map.149), channel_id=1, source_target_pairs={{0,4},{1,5},{2,6},{3,7},{4,0},{5,1},{6,2},{7,3}} | collective-permute-start | bytes 4718600 | tf_op jit(solution)/shard_map/ppermute | solution.py:353
  1001.9 66.5 %collective-permute-start.97 = (bf16[256,3072]{1,0:T(8,128)(2,1)}, bf16[256,3072]{1,0:T(8,128)(2,1)}, u32[]{:S(2)}, u32[]{:S(2)}) collective-permute-start(bf16[256,3072]{1,0:T(8,128)(2,1)} %shard_map.164.refs_0_), channel_id=1, source_target_pairs={{0,2},{1,3},{2,0},{3,1},{4,6},{5,7},{6,4},{7,5}} | collective-permute-start | bytes 4718600 | tf_op jit(solution)/shard_map/ppermute | solution.py:353
  1003.4 52.0 %collective-permute-start.23 = (bf16[128,3072]{1,0:T(8,128)(2,1)}, bf16[128,3072]{1,0:T(8,128)(2,1)}, u32[]{:S(2)}, u32[]{:S(2)}) collective-permute-start(bf16[128,3072]{1,0:T(8,128)(2,1)} %collective-permute-done.21.refs_1_), channel_id=1, source_target_pairs={{0,4},{1,5},{2,6},{3,7},{4,0},{5,1},{6,2},{7,3}} | collective-permute-start | bytes 2359304 | tf_op jit(solution)/shard_map/ppermute | solution.py:353
  1010.5 78.6 %collective-permute-start.98 = (bf16[256,3072]{1,0:T(8,128)(2,1)S(1)}, bf16[256,3072]{1,0:T(8,128)(2,1)}, u32[]{:S(2)}, u32[]{:S(2)}) collective-permute-start(bf16[256,3072]{1,0:T(8,128)(2,1)S(1)} %copy-done.7), channel_id=1, source_target_pairs={{0,4},{1,5},{2,6},{3,7},{4,0},{5,1},{6,2},{7,3}} | collective-permute-start | bytes 4718600 | tf_op jit(solution)/shard_map/ppermute | solution.py:353
  1055.4 67.4 %collective-permute-start.78 = (bf16[256,3072]{1,0:T(8,128)(2,1)}, bf16[256,3072]{1,0:T(8,128)(2,1)}, u32[]{:S(2)}, u32[]{:S(2)}) collective-permute-start(bf16[256,3072]{1,0:T(8,128)(2,1)} %shard_map.157.refs_0_), channel_id=1, source_target_pairs={{0,4},{1,5},{2,6},{3,7},{4,0},{5,1},{6,2},{7,3}} | collective-permute-start | bytes 4718600 | tf_op jit(solution)/shard_map/ppermute | solution.py:353
  1056.3 66.5 %collective-permute-start.79 = (bf16[256,3072]{1,0:T(8,128)(2,1)}, bf16[256,3072]{1,0:T(8,128)(2,1)}, u32[]{:S(2)}, u32[]{:S(2)}) collective-permute-start(bf16[256,3072]{1,0:T(8,128)(2,1)} %shard_map.157.refs_0_), channel_id=1, source_target_pairs={{0,2},{1,3},{2,0},{3,1},{4,6},{5,7},{6,4},{7,5}} | collective-permute-start | bytes 4718600 | tf_op jit(solution)/shard_map/ppermute | solution.py:353
  1068.4 55.3 %collective-permute-start.81 = (bf16[256,3072]{1,0:T(8,128)(2,1)}, bf16[256,3072]{1,0:T(8,128)(2,1)}, u32[]{:S(2)}, u32[]{:S(2)}) collective-permute-start(bf16[256,3072]{1,0:T(8,128)(2,1)} %shard_map.157.refs_0_), channel_id=1, source_target_pairs={{0,1},{1,0},{2,3},{3,2},{4,5},{5,4},{6,7},{7,6}} | collective-permute-start | bytes 4718600 | tf_op jit(solution)/shard_map/ppermute | solution.py:353
  1089.1 42.7 %collective-permute-start.59 = (bf16[256,3072]{1,0:T(8,128)(2,1)}, bf16[256,3072]{1,0:T(8,128)(2,1)}, u32[]{:S(2)}, u32[]{:S(2)}) collective-permute-start(bf16[256,3072]{1,0:T(8,128)(2,1)} %shard_map.150.refs_0_), channel_id=1, source_target_pairs={{0,2},{1,3},{2,0},{3,1},{4,6},{5,7},{6,4},{7,5}} | collective-permute-start | bytes 4718600 | tf_op jit(solution)/shard_map/ppermute | solution.py:353
  1090.6 65.9 %collective-permute-start.60 = (bf16[256,3072]{1,0:T(8,128)(2,1)}, bf16[256,3072]{1,0:T(8,128)(2,1)}, u32[]{:S(2)}, u32[]{:S(2)}) collective-permute-start(bf16[256,3072]{1,0:T(8,128)(2,1)} %shard_map.150.refs_0_), channel_id=1, source_target_pairs={{0,4},{1,5},{2,6},{3,7},{4,0},{5,1},{6,2},{7,3}} | collective-permute-start | bytes 4718600 | tf_op jit(solution)/shard_map/ppermute | solution.py:353
  1122.8 64.3 %collective-permute-start.99 = (bf16[256,3072]{1,0:T(8,128)(2,1)}, bf16[256,3072]{1,0:T(8,128)(2,1)S(1)}, u32[]{:S(2)}, u32[]{:S(2)}) collective-permute-start(bf16[256,3072]{1,0:T(8,128)(2,1)} %collective-permute-done.97.refs_1_), channel_id=1, source_target_pairs={{0,4},{1,5},{2,6},{3,7},{4,0},{5,1},{6,2},{7,3}} | collective-permute-start | bytes 4718600 | tf_op jit(solution)/shard_map/ppermute | solution.py:353
  1123.8 64.3 %collective-permute-start.101 = (bf16[256,3072]{1,0:T(8,128)(2,1)}, bf16[256,3072]{1,0:T(8,128)(2,1)S(1)}, u32[]{:S(2)}, u32[]{:S(2)}) collective-permute-start(bf16[256,3072]{1,0:T(8,128)(2,1)} %collective-permute-done.97.refs_1_), channel_id=1, source_target_pairs={{0,1},{1,0},{2,3},{3,2},{4,5},{5,4},{6,7},{7,6}} | collective-permute-start | bytes 4718600 | tf_op jit(solution)/shard_map/ppermute | solution.py:353
  1131.8 56.5 %collective-permute-start.102 = (bf16[256,3072]{1,0:T(8,128)(2,1)}, bf16[256,3072]{1,0:T(8,128)(2,1)S(1)}, u32[]{:S(2)}, u32[]{:S(2)}) collective-permute-start(bf16[256,3072]{1,0:T(8,128)(2,1)} %collective-permute-done.98.refs_2_), channel_id=1, source_target_pairs={{0,1},{1,0},{2,3},{3,2},{4,5},{5,4},{6,7},{7,6}} | collective-permute-start | bytes 4718600 | tf_op jit(solution)/shard_map/ppermute | solution.py:353
  1188.3 41.8 %collective-permute-start.83 = (bf16[256,3072]{1,0:T(8,128)(2,1)}, bf16[256,3072]{1,0:T(8,128)(2,1)}, u32[]{:S(2)}, u32[]{:S(2)}) collective-permute-start(bf16[256,3072]{1,0:T(8,128)(2,1)} %collective-permute-done.79.refs_2_), channel_id=1, source_target_pairs={{0,1},{1,0},{2,3},{3,2},{4,5},{5,4},{6,7},{7,6}} | collective-permute-start | bytes 4718600 | tf_op jit(solution)/shard_map/ppermute | solution.py:353
  1188.8 41.4 %collective-permute-start.63 = (bf16[256,3072]{1,0:T(8,128)(2,1)}, bf16[256,3072]{1,0:T(8,128)(2,1)}, u32[]{:S(2)}, u32[]{:S(2)}) collective-permute-start(bf16[256,3072]{1,0:T(8,128)(2,1)} %collective-permute-done.59.refs_1_), channel_id=1, source_target_pairs={{0,1},{1,0},{2,3},{3,2},{4,5},{5,4},{6,7},{7,6}} | collective-permute-start | bytes 4718600 | tf_op jit(solution)/shard_map/ppermute | solution.py:353
  1188.8 41.9 %collective-permute-start.64 = (bf16[256,3072]{1,0:T(8,128)(2,1)}, bf16[256,3072]{1,0:T(8,128)(2,1)}, u32[]{:S(2)}, u32[]{:S(2)}) collective-permute-start(bf16[256,3072]{1,0:T(8,128)(2,1)} %collective-permute-done.60.refs_2_), channel_id=1, source_target_pairs={{0,1},{1,0},{2,3},{3,2},{4,5},{5,4},{6,7},{7,6}} | collective-permute-start | bytes 4718600 | tf_op jit(solution)/shard_map/ppermute | solution.py:353
  (86 other events, 2444.5 us)
